TPU v7x, 256 devices: a whole 4x4x8 slice. The times are simulated.
256 devices in a mesh: sample: 16 (over z, y_hi), span: 8 (over x, y_lo), kvhead: 2 (over core).
Axes of the slice: x: 4, y: 4 (y_hi: 2, y_lo: 2; y = y_hi * 2 + y_lo), z: 8, core: 2. Of those that a mesh axis runs over, the one named last changes fastest.
Arguments:
- queries: bfloat16 [16, 256, 3584], P('sample', None, 'kvhead'), may hold values from -6 to 6
- outputs: bfloat16 [16, 256, 3584], P('sample', None, 'kvhead'), may hold values from -6 to 6
- grad_out: bfloat16 [16, 256, 3584], P('sample', None, 'kvhead'), may hold values from -48 to 48
- log_norms: float32 [16, 28, 256], P('sample', 'kvhead'), as said below
- lengths: int32 [16], P('sample'), may hold values from 1 to 256, 1024 in all
- prompt_key_rows: bfloat16 [16384, 512], P(('sample', 'span'), 'kvhead'), may hold values from -9 to 9
- prompt_value_rows: bfloat16 [16384, 512], P(('sample', 'span'), 'kvhead'), may hold values from -6 to 6
- slice_key_rows: bfloat16 [16, 256, 512], P('sample', 'span', 'kvhead'), may hold values from -9 to 9
- slice_value_rows: bfloat16 [16, 256, 512], P('sample', 'span', 'kvhead'), may hold values from -6 to 6
Outputs:
- grad_queries: bfloat16 [16, 256, 3584], P('sample', 'span', 'kvhead')
- grad_k_prompt: bfloat16 [16384, 512], P(('sample', 'span'), 'kvhead')
- grad_v_prompt: bfloat16 [16384, 512], P(('sample', 'span'), 'kvhead')
- grad_k_self: bfloat16 [16, 256, 512], P('sample', 'span', 'kvhead')
- grad_v_self: bfloat16 [16, 256, 512], P('sample', 'span', 'kvhead')
Inputs may be any that keep to these rules, and one draw needn't show every extreme that they name: `log_norms`: every entry lies between 0.8 and 2.4 above the natural logarithm of 16640.
All inputs are finite; a program needn't handle non-finite values. No bound on the sum of `lengths` on one device may be relied on, other than what follows from the above.
Results may differ from a plain program's by a relative error of at most 0.0051.
Values may be sent and summed in bfloat16 or wider, within the bound.
No kernel may reach another device: no remote copies, remote signals or barrier semaphores. Data moves between devices by JAX's collectives and lax.ppermute only.
A program may use at most 64 MiB of HBM per device.

v0:
```python
import math

import jax
import jax.numpy as jnp
from jax import lax
from jax.sharding import Mesh
from jax.sharding import PartitionSpec as P

HEAD_WIDTH = 128
SAMPLE = ("sample_0", "sample_1")
SAMPLE_SPAN = ("sample_0", "sample_1", "span")


def side_by_side(arrays, axis, dim, along):
    widths = [a.shape[along] for a in arrays]
    both = jnp.concatenate(arrays, axis=along)
    whole = lax.all_gather(both, axis, axis=dim, tiled=True)
    return tuple(jnp.split(whole, [sum(widths[:k]) for k in range(1, len(widths))], axis=along))


def summed_rows(running, axes):
    for axis in axes:
        running = lax.psum_scatter(running, axis, scatter_dimension=0, tiled=True)
    return running


def in_blocks(x, dim, size):
    lengths = x.shape
    tiles = x.reshape(*lengths[:dim], size, lengths[dim] // size, *lengths[dim + 1 :])
    return jnp.moveaxis(tiles, dim, 0)


def sent_and_summed(x, axis, dim):
    tiles = in_blocks(x, dim, lax.axis_size(axis))
    arrived = lax.all_to_all(tiles, axis, split_axis=0, concat_axis=0, tiled=True)
    return arrived.sum(axis=0)


def block_size(total_rows, shard_rows):
    block_rows = shard_rows
    while block_rows * 2 <= 512 and total_rows % (block_rows * 2) == 0:
        block_rows = block_rows * 2
    return block_rows


def divide_heads(matrix, head_count):
    return matrix.reshape(matrix.shape[0], head_count, HEAD_WIDTH).transpose(1, 0, 2)


def join_heads(blocks):
    return blocks.transpose(1, 0, 2).reshape(blocks.shape[1], blocks.shape[0] * HEAD_WIDTH)


def shards(
    queries,
    outputs,
    grad_out,
    log_norms,
    lengths,
    prompt_key_rows,
    prompt_value_rows,
    slice_key_rows,
    slice_value_rows,
):
    slice_rows = queries.shape[1]
    kv_local = prompt_key_rows.shape[1] // HEAD_WIDTH
    query_group_width = queries.shape[2] // HEAD_WIDTH // kv_local
    shard_rows = prompt_key_rows.shape[0]
    score_scale = 1.0 / math.sqrt(HEAD_WIDTH)

    def to_groups(input_array):
        return (
            input_array[0]
            .reshape(slice_rows, kv_local, query_group_width, HEAD_WIDTH)
            .transpose(1, 2, 0, 3)
            .reshape(kv_local, query_group_width * slice_rows, HEAD_WIDTH)
        )

    q_rows = to_groups(queries)
    o_rows = to_groups(outputs)
    row_pos = lax.broadcasted_iota(jnp.int32, (query_group_width * slice_rows,), 0) % slice_rows
    live_rows = row_pos < lengths[0]
    g_rows = jnp.where(live_rows[None, :, None], to_groups(grad_out), jnp.zeros((), jnp.bfloat16))
    row_delta = jnp.sum(g_rows.astype(jnp.float32) * o_rows.astype(jnp.float32), axis=-1)
    per_row_norms = log_norms[0].reshape(kv_local, query_group_width * slice_rows)

    def score_terms(key_heads, value_heads, mask):
        scores = (
            jnp.einsum("gqd,gkd->gqk", q_rows, key_heads, preferred_element_type=jnp.float32)
            * score_scale
        )
        prob_rows = jnp.exp(scores - per_row_norms[:, :, None])
        if mask is not None:
            prob_rows = jnp.where(mask[None], prob_rows, 0.0)
        dprobs = jnp.einsum("gqd,gkd->gqk", g_rows, value_heads, preferred_element_type=jnp.float32)
        score_grads = (prob_rows * (dprobs - row_delta[:, :, None])).astype(jnp.bfloat16)
        return (prob_rows.astype(jnp.bfloat16), score_grads)

    def query_term(key_heads, score_grads):
        return (
            jnp.einsum("gqk,gkd->gqd", score_grads, key_heads, preferred_element_type=jnp.float32)
            * score_scale
        )

    def key_terms(prob_low, score_grads):
        key_grad = (
            jnp.einsum("gqk,gqd->gkd", score_grads, q_rows, preferred_element_type=jnp.float32)
            * score_scale
        )
        value_grad = jnp.einsum(
            "gqk,gqd->gkd", prob_low, g_rows, preferred_element_type=jnp.float32
        )
        return (join_heads(key_grad), join_heads(value_grad))

    query_zero = jnp.zeros((kv_local, query_group_width * slice_rows, HEAD_WIDTH), jnp.float32)
    gathered = side_by_side((prompt_key_rows, prompt_value_rows), SAMPLE, 0, 1)
    total_keys = gathered[0].shape[0]
    block_rows = block_size(total_keys, shard_rows)

    def query_step(step_index, query_acc):
        offset = step_index * block_rows
        key_heads = divide_heads(
            lax.dynamic_slice_in_dim(gathered[0], offset, block_rows, 0), kv_local
        )
        value_heads = divide_heads(
            lax.dynamic_slice_in_dim(gathered[1], offset, block_rows, 0), kv_local
        )
        prob_low, score_grads = score_terms(key_heads, value_heads, None)
        return query_acc + query_term(key_heads, score_grads)

    query_prompt = lax.fori_loop(0, total_keys // block_rows, query_step, query_zero)
    inner_rows = block_size(shard_rows * lax.axis_size(SAMPLE), shard_rows)

    def key_step(step_index, state):
        offset = step_index * inner_rows
        key_heads = divide_heads(
            lax.dynamic_slice_in_dim(gathered[0], offset, inner_rows, 0), kv_local
        )
        value_heads = divide_heads(
            lax.dynamic_slice_in_dim(gathered[1], offset, inner_rows, 0), kv_local
        )
        prob_low, score_grads = score_terms(key_heads, value_heads, None)
        key_block, value_block = key_terms(prob_low, score_grads)
        return lax.dynamic_update_slice_in_dim(
            state, jnp.concatenate([key_block, value_block], axis=1), offset, 0
        )

    both_grads = summed_rows(
        lax.fori_loop(
            0,
            shard_rows * lax.axis_size(SAMPLE) // inner_rows,
            key_step,
            jnp.zeros((shard_rows * lax.axis_size(SAMPLE), 2 * kv_local * HEAD_WIDTH), jnp.float32),
        ),
        SAMPLE,
    )
    key_prompt = both_grads[:, : kv_local * HEAD_WIDTH]
    value_prompt = both_grads[:, kv_local * HEAD_WIDTH :]
    self_rows = slice_key_rows.shape[1]
    col_pos = lax.axis_index("span") * self_rows + lax.broadcasted_iota(jnp.int32, (self_rows,), 0)
    visible_mask = col_pos[None, :] <= row_pos[:, None]
    slice_keys = divide_heads(slice_key_rows[0], kv_local)
    slice_values = divide_heads(slice_value_rows[0], kv_local)
    self_prob, self_grads = score_terms(slice_keys, slice_values, visible_mask)
    slice_query_rows = query_term(slice_keys, self_grads)
    slice_key_gradient, slice_value_gradient = key_terms(self_prob, self_grads)
    query_total = query_prompt + slice_query_rows
    flattened_query = (
        query_total.reshape(kv_local, query_group_width, slice_rows, HEAD_WIDTH)
        .transpose(2, 0, 1, 3)
        .reshape(slice_rows, kv_local * query_group_width * HEAD_WIDTH)
    )
    grad_query = sent_and_summed(flattened_query, "span", 0).astype(jnp.bfloat16)
    return (
        grad_query[None],
        key_prompt.astype(jnp.bfloat16),
        value_prompt.astype(jnp.bfloat16),
        slice_key_gradient.astype(jnp.bfloat16)[None],
        slice_value_gradient.astype(jnp.bfloat16)[None],
    )


def solution(mesh):
    split = Mesh(
        mesh.devices.reshape(8, 2, mesh.shape["span"], mesh.shape["kvhead"]),
        ("sample_0", "sample_1", "span", "kvhead"),
    )
    placed = (
        P(SAMPLE, None, "kvhead"),
        P(SAMPLE, None, "kvhead"),
        P(SAMPLE, None, "kvhead"),
        P(SAMPLE, "kvhead", None),
        P(SAMPLE),
        P(SAMPLE_SPAN, "kvhead"),
        P(SAMPLE_SPAN, "kvhead"),
        P(SAMPLE, "span", "kvhead"),
        P(SAMPLE, "span", "kvhead"),
    )
    return jax.shard_map(
        shards,
        mesh=split,
        in_specs=placed,
        out_specs=(
            P(SAMPLE, "span", "kvhead"),
            P(SAMPLE_SPAN, "kvhead"),
            P(SAMPLE_SPAN, "kvhead"),
            P(SAMPLE, "span", "kvhead"),
            P(SAMPLE, "span", "kvhead"),
        ),
        check_vma=False,
    )
```

profile of v0, /device:TPU:8, one launch (start us, length us, event | category | flops | bytes accessed | tf_op | source)
XLA Modules:
  0.0 280.2 jit_solution(5040938324906349694)
XLA Ops:
  11.3 1.5 copy.74
  13.4 1.3 copy.83
  14.7 1.3 copy.78
  16.0 1.5 copy.76
  18.1 1.5 fusion.27
  20.0 1.3 copy.85
  21.3 75.8 %all-gather.2.cloned.1.call-done = bf16[2048,512]{0,1:T(8,128)(2,1)} async-done(((bf16[128,512]{0,1:T(8,128)(2,1)}), bf16[2048,512]{0,1:T(8,128)(2,1)}) %all-gather.2.cloned.1.call-update) | async-done | bytes 2097168 | tf_op jit(solution)/shard_map/all_gather | solution.py:17
  97.1 3.1 %fusion.45 = (bf16[2048,256]{0,1:T(8,128)(2,1)}, bf16[2048,256]{0,1:T(8,128)(2,1)}) fusion(bf16[2048,512]{0,1:T(8,128)(2,1)} %all-gather.2.cloned.1.call-done), kind=kLoop, calls=%fused_computation.69 | loop fusion | bytes 4194304 | tf_op jit(solution)/shard_map/split | solution.py:18
  100.2 2.6 broadcast_in_dim.55.clone
  102.8 76.8 %while.29 = (s32[]{:T(128)}, f32[2048,512]{1,0:T(8,128)}, bf16[2048,256]{0,1:T(8,128)(2,1)}, bf16[2,1792,128]{1,2,0:T(8,128)(2,1)}, f32[1,14,256]{2,1,0:T(8,128)...) while((s32[]{:T(128)}, f32[2048,512]{1,0:T(8,128)}, ...), condition=%wide.wide.region_5.6_spmd, body=%wide.wide.region_4.5_spmd.sunk | while | flops 1894121472 | bytes 35694772 | solution.py:149
  102.8 1.1 constant_dynamic-slice_fusion.8
  104.2 5.2 %fusion.100 = f32[2,512,1792]{2,1,0:T(8,128)} fusion(bf16[2,1792,128]{1,2,0:T(8,128)(2,1)} %get-tuple-element.670, bf16[512,2,128]{2,0,1:T(8,128)(2,1)S(1)} %copy.121), kind=kOutput, calls=%fused_computation.10.clone.clone.1 | convolution fusion | flops 469762048 | bytes 8519680 | tf_op jit(solution)/shard_map/while/body/eval_jaxpr/gqd,gkd->gqk/dot_general | solution.py:89
  109.4 6.3 %fusion.102 = f32[2,512,128]{1,2,0:T(8,128)S(1)} fusion(bf16[2,1792,128]{1,2,0:T(8,128)(2,1)} %get-tuple-element.670, f32[2,512,1792]{2,1,0:T(8,128)} %fusion.100, bf16[2,1792,128]{1,2,0:T(8,128)(2,1)} %get-tuple-element.673, f32[2,1792]{1,0:T(2,128)S(1)} %get-tuple-element.674, f32[2,1792]{1,0:T(2,128)S(1)} %get-tuple-element.675, ...), kind=kOutput, calls=%fused_computation.7.clone.clone.1 | convolution fusion | flops 948830208 | bytes 9990144 | tf_op jit(solution)/shard_map/while/body/eval_jaxpr/gqk,gqd->gkd/dot_general | solution.py:107
  115.7 4.8 %fusion.101 = f32[2,512,128]{1,2,0:T(8,128)S(1)} fusion(bf16[2,1792,128]{1,2,0:T(8,128)(2,1)} %get-tuple-element.673, f32[2,512,1792]{2,1,0:T(8,128)} %fusion.100, f32[2,1792]{1,0:T(2,128)S(1)} %get-tuple-element.675), kind=kOutput, calls=%fused_computation.3.clone.clone.1 | convolution fusion | flops 475267072 | bytes 8796160 | tf_op jit(solution)/shard_map/while/body/eval_jaxpr/gqk,gqd->gkd/dot_general | solution.py:110
  120.9 1.1 constant_dynamic-update-slice_fusion.3
  122.0 1.1 constant_dynamic-slice_fusion.8
  123.4 5.2 %fusion.100 = f32[2,512,1792]{2,1,0:T(8,128)} fusion(bf16[2,1792,128]{1,2,0:T(8,128)(2,1)} %get-tuple-element.670, bf16[512,2,128]{2,0,1:T(8,128)(2,1)S(1)} %copy.121), kind=kOutput, calls=%fused_computation.10.clone.clone.1 | convolution fusion | flops 469762048 | bytes 8519680 | tf_op jit(solution)/shard_map/while/body/eval_jaxpr/gqd,gkd->gqk/dot_general | solution.py:89
  128.6 6.3 %fusion.102 = f32[2,512,128]{1,2,0:T(8,128)S(1)} fusion(bf16[2,1792,128]{1,2,0:T(8,128)(2,1)} %get-tuple-element.670, f32[2,512,1792]{2,1,0:T(8,128)} %fusion.100, bf16[2,1792,128]{1,2,0:T(8,128)(2,1)} %get-tuple-element.673, f32[2,1792]{1,0:T(2,128)S(1)} %get-tuple-element.674, f32[2,1792]{1,0:T(2,128)S(1)} %get-tuple-element.675, ...), kind=kOutput, calls=%fused_computation.7.clone.clone.1 | convolution fusion | flops 948830208 | bytes 9990144 | tf_op jit(solution)/shard_map/while/body/eval_jaxpr/gqk,gqd->gkd/dot_general | solution.py:107
  134.9 4.8 %fusion.101 = f32[2,512,128]{1,2,0:T(8,128)S(1)} fusion(bf16[2,1792,128]{1,2,0:T(8,128)(2,1)} %get-tuple-element.673, f32[2,512,1792]{2,1,0:T(8,128)} %fusion.100, f32[2,1792]{1,0:T(2,128)S(1)} %get-tuple-element.675), kind=kOutput, calls=%fused_computation.3.clone.clone.1 | convolution fusion | flops 475267072 | bytes 8796160 | tf_op jit(solution)/shard_map/while/body/eval_jaxpr/gqk,gqd->gkd/dot_general | solution.py:110
  140.1 1.1 constant_dynamic-update-slice_fusion.3
  141.2 1.1 constant_dynamic-slice_fusion.8
  142.7 5.2 %fusion.100 = f32[2,512,1792]{2,1,0:T(8,128)} fusion(bf16[2,1792,128]{1,2,0:T(8,128)(2,1)} %get-tuple-element.670, bf16[512,2,128]{2,0,1:T(8,128)(2,1)S(1)} %copy.121), kind=kOutput, calls=%fused_computation.10.clone.clone.1 | convolution fusion | flops 469762048 | bytes 8519680 | tf_op jit(solution)/shard_map/while/body/eval_jaxpr/gqd,gkd->gqk/dot_general | solution.py:89
  147.9 6.3 %fusion.102 = f32[2,512,128]{1,2,0:T(8,128)S(1)} fusion(bf16[2,1792,128]{1,2,0:T(8,128)(2,1)} %get-tuple-element.670, f32[2,512,1792]{2,1,0:T(8,128)} %fusion.100, bf16[2,1792,128]{1,2,0:T(8,128)(2,1)} %get-tuple-element.673, f32[2,1792]{1,0:T(2,128)S(1)} %get-tuple-element.674, f32[2,1792]{1,0:T(2,128)S(1)} %get-tuple-element.675, ...), kind=kOutput, calls=%fused_computation.7.clone.clone.1 | convolution fusion | flops 948830208 | bytes 9990144 | tf_op jit(solution)/shard_map/while/body/eval_jaxpr/gqk,gqd->gkd/dot_general | solution.py:107
  154.2 4.8 %fusion.101 = f32[2,512,128]{1,2,0:T(8,128)S(1)} fusion(bf16[2,1792,128]{1,2,0:T(8,128)(2,1)} %get-tuple-element.673, f32[2,512,1792]{2,1,0:T(8,128)} %fusion.100, f32[2,1792]{1,0:T(2,128)S(1)} %get-tuple-element.675), kind=kOutput, calls=%fused_computation.3.clone.clone.1 | convolution fusion | flops 475267072 | bytes 8796160 | tf_op jit(solution)/shard_map/while/body/eval_jaxpr/gqk,gqd->gkd/dot_general | solution.py:110
  160.4 1.1 constant_dynamic-slice_fusion.8
  161.8 5.2 %fusion.100 = f32[2,512,1792]{2,1,0:T(8,128)} fusion(bf16[2,1792,128]{1,2,0:T(8,128)(2,1)} %get-tuple-element.670, bf16[512,2,128]{2,0,1:T(8,128)(2,1)S(1)} %copy.121), kind=kOutput, calls=%fused_computation.10.clone.clone.1 | convolution fusion | flops 469762048 | bytes 8519680 | tf_op jit(solution)/shard_map/while/body/eval_jaxpr/gqd,gkd->gqk/dot_general | solution.py:89
  167.0 6.3 %fusion.102 = f32[2,512,128]{1,2,0:T(8,128)S(1)} fusion(bf16[2,1792,128]{1,2,0:T(8,128)(2,1)} %get-tuple-element.670, f32[2,512,1792]{2,1,0:T(8,128)} %fusion.100, bf16[2,1792,128]{1,2,0:T(8,128)(2,1)} %get-tuple-element.673, f32[2,1792]{1,0:T(2,128)S(1)} %get-tuple-element.674, f32[2,1792]{1,0:T(2,128)S(1)} %get-tuple-element.675, ...), kind=kOutput, calls=%fused_computation.7.clone.clone.1 | convolution fusion | flops 948830208 | bytes 9990144 | tf_op jit(solution)/shard_map/while/body/eval_jaxpr/gqk,gqd->gkd/dot_general | solution.py:107
  173.3 4.8 %fusion.101 = f32[2,512,128]{1,2,0:T(8,128)S(1)} fusion(bf16[2,1792,128]{1,2,0:T(8,128)(2,1)} %get-tuple-element.673, f32[2,512,1792]{2,1,0:T(8,128)} %fusion.100, f32[2,1792]{1,0:T(2,128)S(1)} %get-tuple-element.675), kind=kOutput, calls=%fused_computation.3.clone.clone.1 | convolution fusion | flops 475267072 | bytes 8796160 | tf_op jit(solution)/shard_map/while/body/eval_jaxpr/gqk,gqd->gkd/dot_general | solution.py:110
  181.4 53.3 %while.30 = (s32[]{:T(128)}, f32[2,1792,128]{2,1,0:T(8,128)}, bf16[2048,256]{0,1:T(8,128)(2,1)}, bf16[2,1792,128]{2,1,0:T(8,128)(2,1)S(1)}, f32[1,14,256]{2,1,0:...) while((s32[]{:T(128)}, f32[2,1792,128]{2,1,0:T(8,128)}, ...), condition=%wide.wide.region_2.3_spmd.clone, body=%wide.wide.region_1.2_spmd.clone.sunk | while | flops 1419837440 | bytes 23097536 | solution.py:131
  181.6 1.1 constant_dynamic-slice_fusion.9
  183.1 4.1 %fusion.108 = f32[2,512,1792]{2,1,0:T(8,128)} fusion(bf16[2,1792,128]{2,1,0:T(8,128)(2,1)S(1)} %get-tuple-element.631, bf16[512,2,128]{2,0,1:T(8,128)(2,1)S(1)} %copy.124), kind=kOutput, calls=%fused_computation.22.clone.clone.1 | convolution fusion | flops 469762048 | bytes 8519680 | tf_op jit(solution)/shard_map/while/body/eval_jaxpr/gqd,gkd->gqk/dot_general | solution.py:89
  187.1 7.6 %fusion.109 = f32[2,1792,128]{2,1,0:T(8,128)} fusion(f32[2,1792,128]{2,1,0:T(8,128)} %get-tuple-element.616, f32[2,512,1792]{2,1,0:T(8,128)} %fusion.108, bf16[2,1792,128]{2,1,0:T(8,128)(2,1)S(1)} %get-tuple-element.634, f32[2,1792]{1,0:T(2,128)S(1)} %get-tuple-element.635, f32[2,1792]{1,0:T(2,128)S(1)} %get-tuple-element.636, ...), kind=kOutput, calls=%fused_computation.19.clone.clone.1 | convolution fusion | flops 950075392 | bytes 12480513 | tf_op jit(solution)/shard_map/while/body/eval_jaxpr/gqk,gkd->gqd/dot_general | solution.py:101
  194.7 1.1 constant_dynamic-slice_fusion.9
  196.2 4.1 %fusion.108 = f32[2,512,1792]{2,1,0:T(8,128)} fusion(bf16[2,1792,128]{2,1,0:T(8,128)(2,1)S(1)} %get-tuple-element.631, bf16[512,2,128]{2,0,1:T(8,128)(2,1)S(1)} %copy.124), kind=kOutput, calls=%fused_computation.22.clone.clone.1 | convolution fusion | flops 469762048 | bytes 8519680 | tf_op jit(solution)/shard_map/while/body/eval_jaxpr/gqd,gkd->gqk/dot_general | solution.py:89
  200.2 7.8 %fusion.109 = f32[2,1792,128]{2,1,0:T(8,128)} fusion(f32[2,1792,128]{2,1,0:T(8,128)} %get-tuple-element.616, f32[2,512,1792]{2,1,0:T(8,128)} %fusion.108, bf16[2,1792,128]{2,1,0:T(8,128)(2,1)S(1)} %get-tuple-element.634, f32[2,1792]{1,0:T(2,128)S(1)} %get-tuple-element.635, f32[2,1792]{1,0:T(2,128)S(1)} %get-tuple-element.636, ...), kind=kOutput, calls=%fused_computation.19.clone.clone.1 | convolution fusion | flops 950075392 | bytes 12480513 | tf_op jit(solution)/shard_map/while/body/eval_jaxpr/gqk,gkd->gqd/dot_general | solution.py:101
  208.1 1.1 constant_dynamic-slice_fusion.9
  209.5 4.1 %fusion.108 = f32[2,512,1792]{2,1,0:T(8,128)} fusion(bf16[2,1792,128]{2,1,0:T(8,128)(2,1)S(1)} %get-tuple-element.631, bf16[512,2,128]{2,0,1:T(8,128)(2,1)S(1)} %copy.124), kind=kOutput, calls=%fused_computation.22.clone.clone.1 | convolution fusion | flops 469762048 | bytes 8519680 | tf_op jit(solution)/shard_map/while/body/eval_jaxpr/gqd,gkd->gqk/dot_general | solution.py:89
  213.6 7.9 %fusion.109 = f32[2,1792,128]{2,1,0:T(8,128)} fusion(f32[2,1792,128]{2,1,0:T(8,128)} %get-tuple-element.616, f32[2,512,1792]{2,1,0:T(8,128)} %fusion.108, bf16[2,1792,128]{2,1,0:T(8,128)(2,1)S(1)} %get-tuple-element.634, f32[2,1792]{1,0:T(2,128)S(1)} %get-tuple-element.635, f32[2,1792]{1,0:T(2,128)S(1)} %get-tuple-element.636, ...), kind=kOutput, calls=%fused_computation.19.clone.clone.1 | convolution fusion | flops 950075392 | bytes 12480513 | tf_op jit(solution)/shard_map/while/body/eval_jaxpr/gqk,gkd->gqd/dot_general | solution.py:101
  221.4 1.1 constant_dynamic-slice_fusion.9
  222.8 4.1 %fusion.108 = f32[2,512,1792]{2,1,0:T(8,128)} fusion(bf16[2,1792,128]{2,1,0:T(8,128)(2,1)S(1)} %get-tuple-element.631, bf16[512,2,128]{2,0,1:T(8,128)(2,1)S(1)} %copy.124), kind=kOutput, calls=%fused_computation.22.clone.clone.1 | convolution fusion | flops 469762048 | bytes 8519680 | tf_op jit(solution)/shard_map/while/body/eval_jaxpr/gqd,gkd->gqk/dot_general | solution.py:89
  226.9 7.8 %fusion.109 = f32[2,1792,128]{2,1,0:T(8,128)} fusion(f32[2,1792,128]{2,1,0:T(8,128)} %get-tuple-element.616, f32[2,512,1792]{2,1,0:T(8,128)} %fusion.108, bf16[2,1792,128]{2,1,0:T(8,128)(2,1)S(1)} %get-tuple-element.634, f32[2,1792]{1,0:T(2,128)S(1)} %get-tuple-element.635, f32[2,1792]{1,0:T(2,128)S(1)} %get-tuple-element.636, ...), kind=kOutput, calls=%fused_computation.19.clone.clone.1 | convolution fusion | flops 950075392 | bytes 12480513 | tf_op jit(solution)/shard_map/while/body/eval_jaxpr/gqk,gkd->gqd/dot_general | solution.py:101
  234.7 2.0 fusion.20
  236.7 2.4 copy.110
  239.1 2.7 reshape_reshape.3
  241.8 5.7 %all-to-all-start = ((f32[8,32,1792]{2,1,0:T(8,128)}), f32[8,32,1792]{2,1,0:T(8,128)}, u32[]{:S(2)}, u32[]{:S(2)}) async-start(f32[8,32,1792]{2,1,0:T(8,128)} %reshape_reshape.3), calls=%async_computation | async-start | bytes 3670016 | tf_op jit(solution)/shard_map/all_to_all | solution.py:35
  250.0 18.3 %all-to-all-done = f32[8,32,1792]{2,1,0:T(8,128)} async-done(((f32[8,32,1792]{2,1,0:T(8,128)}), f32[8,32,1792]{2,1,0:T(8,128)}, u32[]{:S(2)}, u32[]{:S(2)}) %all-to-all-start) | async-done | bytes 1835040 | tf_op jit(solution)/shard_map/all_to_all | solution.py:35
  268.3 2.3 reduce_sum.22
  270.6 1.4 reduce-scatter.5.cloned.1.call-done
  (79 shorter events, 17.3 us)
Async XLA Ops:
  7.2 7.5 %copy-start.2 = (bf16[1,256,1792]{2,1,0:T(8,128)(2,1)S(1)}, bf16[1,256,1792]{2,1,0:T(8,128)(2,1)}, u32[]{:S(2)}) copy-start(bf16[1,256,1792]{2,1,0:T(8,128)(2,1)} %param.14) | copy-start | bytes 2752516
  7.2 89.9 %all-gather.2.cloned.1.call-start = ((), (), s32[]{:S(2)}) async-start(), calls=%async_computation.3 | async-start | bytes 2228224 | tf_op jit(solution)/shard_map/all_gather | solution.py:17
  9.9 237.6 %reduce-scatter.3.cloned.1.call-start = ((), (), s32[]{:S(2)}) async-start(), calls=%async_computation.4 | async-start | bytes 4718592 | tf_op jit(solution)/shard_map/reduce_scatter | solution.py:23
  11.3 6.2 %copy-start.3 = (f32[1,14,256]{2,1,0:T(8,128)}, f32[1,14,256]{2,1,0:T(8,128)S(1)}, u32[]{:S(2)}) copy-start(f32[1,14,256]{2,1,0:T(8,128)S(1)} %copy.79) | copy-start | bytes 43012
  20.0 82.8 %copy-start = (bf16[2,1792,128]{2,1,0:T(8,128)(2,1)}, bf16[2,1792,128]{2,1,0:T(8,128)(2,1)S(1)}, u32[]{:S(2)}) copy-start(bf16[2,1792,128]{2,1,0:T(8,128)(2,1)S(1)} %bitcast_select_fusion) | copy-start | bytes 2752516
  179.5 0.7 copy-start.4
  179.5 0.7 copy-start.6
  179.5 0.8 copy-start.7
  179.6 0.8 copy-start.5
  179.6 1.4 copy-start.1
  241.8 26.5 %all-to-all-start = ((f32[8,32,1792]{2,1,0:T(8,128)}), f32[8,32,1792]{2,1,0:T(8,128)}, u32[]{:S(2)}, u32[]{:S(2)}) async-start(f32[8,32,1792]{2,1,0:T(8,128)} %reshape_reshape.3), calls=%async_computation | async-start | bytes 3670016 | tf_op jit(solution)/shard_map/all_to_all | solution.py:35
  247.5 24.5 %reduce-scatter.5.cloned.1.call-start = ((), (), s32[]{:S(2)}) async-start(), calls=%async_computation.5 | async-start | bytes 786432 | tf_op jit(solution)/shard_map/reduce_scatter | solution.py:23
Sparse Core Ops, SparseCore 0:
  10.5 86.5 all-gather.1
  179.7 52.8 reduce-scatter.2
  250.8 21.1 reduce-scatter.4
where the time goes:
time: 281 us; the launch traced here: 280 us
  matrix products  116 us (41%)
  waiting for transfers between devices  96.2 us (34%)
  local copies, waits for them, and re-layouts  41.2 us (15%)
  between operations  14.7 us (5%)
  other arithmetic  6.19 us (2%)
  starting transfers between devices  5.79 us (2%)
    all_gather x1, waiting for transfers between devices, side_by_side(): whole = lax.all_gather(both, axis, axis=dim, tiled=True)  75.8 us
    dot_general x9, matrix products, score_terms(): jnp.einsum('gqd,gkd->gqk', q_rows, key_heads, preferred_element_type=jnp....  37.5 us
    dot_general x5, matrix products, query_term(): jnp.einsum('gqk,gkd->gqd', score_grads, key_heads, preferred_element_type...  33.1 us
    dot_general x5, matrix products, key_terms(): jnp.einsum('gqk,gqd->gkd', score_grads, q_rows, preferred_element_type=jn...  25.4 us
    dot_general x5, matrix products, key_terms(): jnp.einsum('gqk,gqd->gkd', prob_low, g_rows, preferred_element_type=jnp.f...  19.3 us
    all_to_all x1, waiting for transfers between devices, sent_and_summed(): lax.all_to_all(tiles, axis, split_axis=0, concat_axis=0, tiled=True)  18.3 us
    unnamed x22, local copies, waits for them, and re-layouts  6.88 us
    all_to_all x1, starting transfers between devices, sent_and_summed(): lax.all_to_all(tiles, axis, split_axis=0, concat_axis=0, tiled=True)  5.71 us
  transfers between devices with their start and end apart: 4, of which 3 were waited for; matrix products, arithmetic and copies ran while one was open for 27% of the time, Pallas kernels for 0%

commit v1 on v0

v1 whole, which is shorter than its diff:
```python
import math

import jax
import jax.numpy as jnp
from jax import lax
from jax.experimental import pallas as pl
from jax.experimental.pallas import tpu as pltpu
from jax.sharding import Mesh
from jax.sharding import PartitionSpec as P

HEAD_WIDTH = 128
SAMPLE = ("sample_0", "sample_1")
PLANE = ("sample_1", "span")
SAMPLE_SPAN = ("sample_0", "sample_1", "span")
GROUP = 7
CLASSES = 8
SLOTS = 18
INTERPRET = False
BF16 = jnp.bfloat16
F32 = jnp.float32
SCALE = 1.0 / math.sqrt(HEAD_WIDTH)


def exchange(tiles, axes):
    return lax.all_to_all(tiles, axes, split_axis=0, concat_axis=0, tiled=True)


def dot(a, b, ca, cb):
    return lax.dot_general(a, b, (((ca,), (cb,)), ((), ())), preferred_element_type=F32)


def call(body, out_shape, *args, **kw):
    return pl.pallas_call(body, out_shape=out_shape, interpret=INTERPRET, **kw)(*args)


def pick_kernel(info, q_ref, g_ref, out_ref):
    p, off, live = info[0], info[1], info[2]
    shape = (64, 512)
    row = lax.broadcasted_iota(jnp.int32, shape, 0)
    col = lax.broadcasted_iota(jnp.int32, shape, 1)
    i = col % 256
    hit = (
        (i % CLASSES == p)
        & (i < live)
        & ((off + i // CLASSES) % 8 == row // 8)
        & (i // 64 == row % 4)
        & (col // 256 == (row // 4) % 2)
    )
    pick = jnp.where(hit, 1.0, 0.0).astype(BF16)
    for head in range(2 * GROUP):
        lanes = slice(head * HEAD_WIDTH, (head + 1) * HEAD_WIDTH)
        both = jnp.concatenate([q_ref[:, lanes], g_ref[:, lanes]], axis=0)
        rows = dot(pick, both, 1, 0).astype(BF16)
        out_ref[:, head // GROUP, head % GROUP] = rows.reshape(8, 8, HEAD_WIDTH)


def place_kernel(dest_ref, rows_ref, out_ref):
    total = out_ref.shape[0]
    dest = dest_ref[0:1, :]
    hit = lax.broadcasted_iota(jnp.int32, (total, dest.shape[1]), 0) == dest
    out_ref[...] = dot(jnp.where(hit, 1.0, 0.0).astype(BF16), rows_ref[...], 1, 0).astype(BF16)


def place(dest, rows, total):
    return call(
        place_kernel, jax.ShapeDtypeStruct((total, HEAD_WIDTH), BF16), dest[None, :], rows
    )


def sum_place_kernel(dest_ref, parts_ref, out_ref):
    total = out_ref.shape[0]
    rows = parts_ref[0].astype(F32)
    for k in range(1, parts_ref.shape[0]):
        rows = rows + parts_ref[k].astype(F32)
    hit = lax.broadcasted_iota(jnp.int32, (rows.shape[0], total), 0) == dest_ref[0:1, :]
    pick = jnp.where(hit, 1.0, 0.0).astype(BF16)
    out_ref[...] = dot(pick, rows.astype(BF16), 0, 0).astype(BF16)


def prompt_kernel(kv_ref, rows_ref, norm_ref, kvg_ref, gq_ref, acc_ref):
    step = pl.program_id(0)

    @pl.when(step == 0)
    def _():
        acc_ref[...] = jnp.zeros_like(acc_ref)

    keys = kv_ref[:, 0:128, :].reshape(-1, HEAD_WIDTH)
    values = kv_ref[:, 128:256, :].reshape(-1, HEAD_WIDTH)
    gk = jnp.zeros(keys.shape, F32)
    gv = jnp.zeros(keys.shape, F32)
    for part in range(4):
        q = rows_ref[2 * part : 2 * part + 2, 0:128, :].reshape(256, HEAD_WIDTH)
        g = rows_ref[2 * part : 2 * part + 2, 128:256, :].reshape(256, HEAD_WIDTH)
        lanes = slice(256 * part, 256 * part + 256)
        prob = jnp.exp(dot(keys, q, 1, 1) * SCALE - norm_ref[0:1, lanes])
        sgrad = (prob * (dot(values, g, 1, 1) - norm_ref[1:2, lanes])).astype(BF16)
        gv = gv + dot(prob.astype(BF16), g, 1, 0)
        gk = gk + dot(sgrad, q, 1, 0)
        acc_ref[lanes, :] += dot(sgrad, keys, 0, 0)
    kvg_ref[:, 0:128, :] = (gk * SCALE).astype(BF16).reshape(-1, 128, HEAD_WIDTH)
    kvg_ref[:, 128:256, :] = gv.astype(BF16).reshape(-1, 128, HEAD_WIDTH)

    @pl.when(step == pl.num_programs(0) - 1)
    def _():
        gq_ref[...] = (acc_ref[...] * SCALE).astype(BF16)


def prompt_terms(kv, rows, norms):
    sources = kv.shape[0]
    per = 2
    block = pl.BlockSpec((per, 256, HEAD_WIDTH), lambda k: (k, 0, 0))
    return pl.pallas_call(
        prompt_kernel,
        grid=(sources // per,),
        in_specs=[
            block,
            pl.BlockSpec(rows.shape, lambda k: (0, 0, 0)),
            pl.BlockSpec(norms.shape, lambda k: (0, 0)),
        ],
        out_specs=[block, pl.BlockSpec((1024, HEAD_WIDTH), lambda k: (0, 0))],
        out_shape=[
            jax.ShapeDtypeStruct(kv.shape, BF16),
            jax.ShapeDtypeStruct((1024, HEAD_WIDTH), BF16),
        ],
        scratch_shapes=[pltpu.VMEM((1024, HEAD_WIDTH), F32)],
        interpret=INTERPRET,
    )(kv, rows, norms)


def key_sum_kernel(parts_ref, k_ref, v_ref):
    for head in range(2):
        total = parts_ref[head, 0].astype(F32)
        for k in range(1, parts_ref.shape[1]):
            total = total + parts_ref[head, k].astype(F32)
        lanes = slice(head * HEAD_WIDTH, (head + 1) * HEAD_WIDTH)
        k_ref[:, lanes] = total[0:128].astype(BF16)
        v_ref[:, lanes] = total[128:256].astype(BF16)


def self_kernel(
    info, q_ref, g_ref, norm_ref, delta_ref, col_norm_ref, col_delta_ref, own_ref, kv_ref,
    gk_ref, gv_ref, gq_ref,
):
    p, live = info[0], info[1]
    rows_total = q_ref.shape[0]
    i_row = lax.broadcasted_iota(jnp.int32, (32, rows_total), 1)
    j_row = lax.broadcasted_iota(jnp.int32, (32, rows_total), 0) + p * 32
    live_row = lax.broadcasted_iota(jnp.int32, (rows_total, HEAD_WIDTH), 0) < live
    live_own = lax.broadcasted_iota(jnp.int32, (32, HEAD_WIDTH), 0) + p * 32 < live
    zero = jnp.zeros((), BF16)
    for kv in range(2):
        key_lanes = slice(kv * HEAD_WIDTH, (kv + 1) * HEAD_WIDTH)
        value_lanes = slice((kv + 2) * HEAD_WIDTH, (kv + 3) * HEAD_WIDTH)
        keys, values = own_ref[:, key_lanes], own_ref[:, value_lanes]
        all_keys = kv_ref[:, :, key_lanes].reshape(rows_total, HEAD_WIDTH)
        all_values = kv_ref[:, :, value_lanes].reshape(rows_total, HEAD_WIDTH)
        gk = jnp.zeros((32, HEAD_WIDTH), F32)
        gv = jnp.zeros((32, HEAD_WIDTH), F32)
        for inner in range(GROUP):
            head = kv * GROUP + inner
            lanes = slice(head * HEAD_WIDTH, (head + 1) * HEAD_WIDTH)
            q = q_ref[:, lanes]
            g = jnp.where(live_row, g_ref[:, lanes], zero)
            prob = jnp.exp(dot(keys, q, 1, 1) * SCALE - norm_ref[head : head + 1, :])
            prob = jnp.where(j_row <= i_row, prob, 0.0)
            sgrad = prob * (dot(values, g, 1, 1) - delta_ref[head : head + 1, :])
            gv = gv + dot(prob.astype(BF16), g, 1, 0)
            gk = gk + dot(sgrad.astype(BF16), q, 1, 0)
            q_own = q_ref[pl.ds(pl.multiple_of(p * 32, 32), 32), lanes]
            g_own = g_ref[pl.ds(pl.multiple_of(p * 32, 32), 32), lanes]
            g_own = jnp.where(live_own, g_own, zero)
            prob = jnp.exp(dot(q_own, all_keys, 1, 1) * SCALE - col_norm_ref[:, head : head + 1])
            i_own = lax.broadcasted_iota(jnp.int32, prob.shape, 0) + p * 32
            prob = jnp.where(lax.broadcasted_iota(jnp.int32, prob.shape, 1) <= i_own, prob, 0.0)
            sgrad = prob * (dot(g_own, all_values, 1, 1) - col_delta_ref[:, head : head + 1])
            gq_ref[:, lanes] = dot(sgrad.astype(BF16), all_keys, 1, 0) * SCALE
        gk_ref[:, key_lanes] = (gk * SCALE).astype(BF16)
        gv_ref[:, key_lanes] = gv.astype(BF16)


def shards(
    queries,
    outputs,
    grad_out,
    log_norms,
    lengths,
    prompt_key_rows,
    prompt_value_rows,
    slice_key_rows,
    slice_value_rows,
):
    z = lax.axis_index("sample_0")
    half = lax.axis_index("sample_1")
    p = lax.axis_index("span")
    sample = 2 * z + half
    spans = lax.axis_size("span")
    slice_rows = queries.shape[1]
    heads = queries.shape[2] // HEAD_WIDTH
    q, o, g = queries[0], outputs[0], grad_out[0]
    norms = log_norms[0]
    live = lengths[0]

    kv_heads = jnp.concatenate(
        [
            prompt_key_rows.reshape(-1, 2, HEAD_WIDTH).transpose(1, 0, 2),
            prompt_value_rows.reshape(-1, 2, HEAD_WIDTH).transpose(1, 0, 2),
        ],
        axis=1,
    )
    kv_send = jnp.broadcast_to(kv_heads[:, None], (2, spans, *kv_heads.shape[1:]))
    kv = exchange(kv_send.reshape(2 * spans, *kv_heads.shape[1:]), PLANE)

    live_rows = lax.broadcasted_iota(jnp.int32, (slice_rows, 1), 0) < live
    g_live = jnp.where(live_rows, g, jnp.zeros((), BF16))
    delta = jnp.sum(
        (g_live.astype(F32) * o.astype(F32)).reshape(slice_rows, heads, HEAD_WIDTH), axis=-1
    ).T
    class_rows = slice_rows // CLASSES

    def of_class(x):
        return lax.dynamic_index_in_dim(x.reshape(heads, class_rows, CLASSES), p, 2, keepdims=False)

    stats = jnp.stack([of_class(norms), of_class(delta)])
    stats = stats.reshape(2, 2, GROUP * class_rows).transpose(1, 0, 2)
    stats = jnp.concatenate(
        [
            stats.reshape(2, 2 * GROUP * class_rows),
            jnp.broadcast_to(live.astype(F32), (2, 512 - 2 * GROUP * class_rows)),
        ],
        axis=1,
    )
    stats = exchange(jnp.broadcast_to(stats[None], (8, 2, 512)).reshape(16, 512), SAMPLE)
    all_lengths = stats[:, 2 * GROUP * class_rows].astype(jnp.int32)
    live_of = jnp.clip((all_lengths - p + CLASSES - 1) // CLASSES, 0, class_rows)
    before = lax.broadcasted_iota(jnp.int32, (16, 16), 1) < lax.broadcasted_iota(
        jnp.int32, (16, 16), 0
    )
    offset = jnp.sum(jnp.where(before, live_of[None, :], 0), axis=1)
    own_offset = jnp.sum(jnp.where(jnp.arange(16) == sample, offset, 0))

    picked = call(
        pick_kernel,
        jax.ShapeDtypeStruct((8, 2, GROUP, 8, HEAD_WIDTH), BF16),
        jnp.stack([p, own_offset, live]),
        q,
        g,
        in_specs=[
            pl.BlockSpec(memory_space=pltpu.SMEM),
            pl.BlockSpec(memory_space=pltpu.VMEM),
            pl.BlockSpec(memory_space=pltpu.VMEM),
        ],
    )
    arrived = exchange(picked.reshape(16, GROUP * 8, HEAD_WIDTH), SAMPLE)
    step4 = jnp.arange(4)[None, :]
    local = 8 * step4 + ((z - offset) % 8)[:, None]
    slot = jnp.where(local < live_of[:, None], (offset[:, None] + local) // 8, -4096)
    compact_dest = (
        slot[:, None, None, :]
        + SLOTS * jnp.arange(GROUP)[None, :, None, None]
        + 128 * jnp.arange(2)[None, None, :, None]
    )
    compact = place(compact_dest.reshape(-1), arrived.reshape(-1, HEAD_WIDTH), 256)
    rows = exchange(jnp.broadcast_to(compact[None], (8, 256, HEAD_WIDTH)), "sample_0")

    rank = 8 * jnp.arange(SLOTS)[None, :] + jnp.arange(8)[:, None]
    in_class = jnp.arange(class_rows)[None, :]
    rank_of = jnp.where(in_class < live_of[:, None], offset[:, None] + in_class, -1)
    chosen = (rank_of.reshape(-1)[:, None] == rank.reshape(-1)[None, :]).astype(F32)
    table = stats[:, : 2 * GROUP * class_rows].reshape(16, 2 * GROUP, class_rows)
    table = table.transpose(1, 0, 2).reshape(2 * GROUP, 16 * class_rows)
    row_stats = jnp.dot(table, chosen, precision=lax.Precision.HIGHEST)
    row_stats = row_stats.reshape(2, GROUP, 8, SLOTS).transpose(0, 2, 1, 3)
    row_stats = jnp.pad(
        row_stats.reshape(2, 8, GROUP * SLOTS), ((0, 0), (0, 0), (0, 128 - GROUP * SLOTS))
    ).reshape(2, 1024)

    own_kv = jnp.concatenate([slice_key_rows[0], slice_value_rows[0]], axis=1)
    slice_kv = exchange(jnp.broadcast_to(own_kv[None], (spans, *own_kv.shape)), "span")
    own_rows = slice_rows // spans
    col_norms = lax.dynamic_slice_in_dim(norms, p * own_rows, own_rows, 1).T
    col_delta = lax.dynamic_slice_in_dim(delta, p * own_rows, own_rows, 1).T
    own_shape = jax.ShapeDtypeStruct((own_rows, 2 * HEAD_WIDTH), BF16)
    gk_self, gv_self, gq_self = call(
        self_kernel,
        [own_shape, own_shape, jax.ShapeDtypeStruct((own_rows, heads * HEAD_WIDTH), F32)],
        jnp.stack([p, live]),
        q,
        g,
        norms,
        delta,
        col_norms,
        col_delta,
        own_kv,
        slice_kv,
        in_specs=[pl.BlockSpec(memory_space=pltpu.SMEM)]
        + [pl.BlockSpec(memory_space=pltpu.VMEM)] * 8,
    )

    kv_grads, gq_part = prompt_terms(kv, rows, row_stats)
    kv_parts = exchange(kv_grads, PLANE)
    prompt_shape = jax.ShapeDtypeStruct(prompt_key_rows.shape, BF16)
    gk_prompt, gv_prompt = call(
        key_sum_kernel,
        [prompt_shape, prompt_shape],
        kv_parts.reshape(2, spans, *kv_parts.shape[1:]),
    )

    gq_parts = exchange(gq_part.reshape(8, 128, HEAD_WIDTH), "sample_0")
    back = slot[:, None, :] + SLOTS * jnp.arange(8)[None, :, None]
    back = jnp.where(jnp.arange(8)[None, :, None] < GROUP, back, -1)
    returned = call(
        sum_place_kernel,
        jax.ShapeDtypeStruct((512, HEAD_WIDTH), BF16),
        back.reshape(1, 512),
        gq_parts,
    )
    returned = exchange(returned.reshape(16, 32, HEAD_WIDTH), SAMPLE)
    index = jnp.arange(512)
    from_z, from_head = index // 64, GROUP * ((index // 32) % 2) + (index % 32) // 4
    in_class = 8 * (index % 4) + (from_z - own_offset) % 8
    spread_dest = (in_class // 4) * (heads * 4) + from_head * 4 + in_class % 4
    spread_dest = jnp.where((index % 32) // 4 < GROUP, spread_dest, -1)
    spread = place(spread_dest, returned.reshape(512, HEAD_WIDTH), heads * slice_rows // CLASSES)
    final = exchange(spread.reshape(spans, heads * 4, HEAD_WIDTH), "span")
    gq_prompt = final.reshape(CLASSES, heads, 4, HEAD_WIDTH).transpose(2, 0, 1, 3)
    grad_query = (gq_prompt.reshape(own_rows, heads * HEAD_WIDTH).astype(F32) + gq_self).astype(BF16)
    return grad_query[None], gk_prompt, gv_prompt, gk_self[None], gv_self[None]


def solution(mesh):
    split = Mesh(
        mesh.devices.reshape(8, 2, mesh.shape["span"], mesh.shape["kvhead"]),
        ("sample_0", "sample_1", "span", "kvhead"),
    )
    placed = (
        P(SAMPLE, None, "kvhead"),
        P(SAMPLE, None, "kvhead"),
        P(SAMPLE, None, "kvhead"),
        P(SAMPLE, "kvhead", None),
        P(SAMPLE),
        P(SAMPLE_SPAN, "kvhead"),
        P(SAMPLE_SPAN, "kvhead"),
        P(SAMPLE, "span", "kvhead"),
        P(SAMPLE, "span", "kvhead"),
    )
    return jax.shard_map(
        shards,
        mesh=split,
        in_specs=placed,
        out_specs=(
            P(SAMPLE, "span", "kvhead"),
            P(SAMPLE_SPAN, "kvhead"),
            P(SAMPLE_SPAN, "kvhead"),
            P(SAMPLE, "span", "kvhead"),
            P(SAMPLE, "span", "kvhead"),
        ),
        check_vma=False,
    )
```

time: 281 us -> 174 us (0.62)
  matrix products: 116 us -> 0.69 us
  starting transfers between devices: 5.79 us -> 39.3 us
  Pallas kernels: 0 us -> 29.6 us
  local copies, waits for them, and re-layouts: 41.2 us -> 14.7 us
  waiting for transfers between devices: 96.2 us -> 70.5 us
  between operations: 14.7 us -> 1.7 us
  blocking collectives: 0 us -> 9.41 us
    dot_general x25 -> x1, matrix products: 116 us -> 0.69 us  [shards(): row_stats = jnp.dot(table, chosen, precision=lax.Precision.HIGHEST)]
    all_gather x1 -> x0, waiting for transfers between devices: 75.8 us -> none  [side_by_side(): whole = lax.all_gather(both, axis, axis=dim, tiled=True)]
    all_to_all x1 -> x8, waiting for transfers between devices: 18.3 us -> 70.5 us  [exchange(): return lax.all_to_all(tiles, axes, split_axis=0, concat_axis=0, tiled=True)]
    all_to_all x1 -> x8, starting transfers between devices: 5.71 us -> 39.3 us  [exchange(): return lax.all_to_all(tiles, axes, split_axis=0, concat_axis=0, tiled=True)]
    pallas_call x0 -> x7, Pallas kernels: none -> 29.6 us  [the longest x6 16.6 us: call(): pl.pallas_call(body, out_shape=out_shape, interpret=INTERPRET, **kw)(*args)]
    all_to_all x0 -> x1, blocking collectives: none -> 9.41 us  [exchange(): return lax.all_to_all(tiles, axes, split_axis=0, concat_axis=0, tiled=True)]
    dynamic_slice x8 -> x3, local copies, waits for them, and re-layouts: 8.55 us -> 1.13 us  [the longest x2 0.78 us: shards(): col_norms = lax.dynamic_slice_in_dim(norms, p * own_rows, own_rows, 1).T]
    dynamic_update_slice x8 -> x0, local copies, waits for them, and re-layouts: 5.65 us -> none  [key_step(): lax.dynamic_update_slice_in_dim(state, jnp.concatenate([key_block, value_...]
  transfers between devices with their start and end apart: 4 -> 8, of which waited for: 3 -> 8; matrix products, arithmetic and copies ran while one was open for 27% -> 6% of each run, Pallas kernels for 0% -> 6%
where the time goes in v1:
time: 174 us; the launch traced here: 173 us
  waiting for transfers between devices  70.5 us (41%)
  starting transfers between devices  39.3 us (23%)
  Pallas kernels  29.6 us (17%)
  local copies, waits for them, and re-layouts  14.7 us (8%)
  blocking collectives  9.41 us (5%)
  other arithmetic  6.69 us (4%)
    all_to_all x8, waiting for transfers between devices, exchange(): return lax.all_to_all(tiles, axes, split_axis=0, concat_axis=0, tiled=True)  70.5 us
    all_to_all x8, starting transfers between devices, exchange(): return lax.all_to_all(tiles, axes, split_axis=0, concat_axis=0, tiled=True)  39.3 us
    pallas_call x6, Pallas kernels, call(): pl.pallas_call(body, out_shape=out_shape, interpret=INTERPRET, **kw)(*args)  16.6 us
    pallas_call x1, Pallas kernels, prompt_terms(): pl.pallas_call(prompt_kernel, grid=(sources // per,), in_specs=[block, pl...  13 us
    all_to_all x1, blocking collectives, exchange(): return lax.all_to_all(tiles, axes, split_axis=0, concat_axis=0, tiled=True)  9.41 us
    unnamed x37, local copies, waits for them, and re-layouts  6.64 us
  transfers between devices with their start and end apart: 8, of which 8 were waited for; matrix products, arithmetic and copies ran while one was open for 6% of the time, Pallas kernels for 6%

profile of v1, /device:TPU:8, one launch (start us, length us, event | category | flops | bytes accessed | tf_op | source)
XLA Modules:
  0.0 172.5 jit_solution(15995086568030896726)
XLA Ops:
  1.4 1.5 copy.58
  2.9 0.5 copy.59
  3.4 0.3 fusion
  3.9 0.2 copy-done.10
  4.3 0.4 dynamic-slice_reduce_fusion
  5.0 0.7 all_to_all.43
  5.6 10.3 %all-to-all-start = ((f32[16,1,512]{2,1,0:T(1,128)}), f32[16,1,512]{2,1,0:T(1,128)S(1)}, u32[]{:S(2)}, u32[]{:S(2)}) async-start(f32[16,1,512]{2,1,0:T(1,128)} %all_to_all.43), calls=%async_computation | async-start | bytes 65536 | tf_op jit(solution)/shard_map/all_to_all | solution.py:25
  15.9 10.3 %all-to-all-done = f32[16,1,512]{2,1,0:T(1,128)S(1)} async-done(((f32[16,1,512]{2,1,0:T(1,128)}), f32[16,1,512]{2,1,0:T(1,128)S(1)}, u32[]{:S(2)}, u32[]{:S(2)}) %all-to-all-start) | async-done | bytes 32800 | tf_op jit(solution)/shard_map/all_to_all | solution.py:25
  26.5 0.6 and_select_fusion.9
  27.2 1.2 pad_add_fusion.info
  28.4 2.6 %shard_map.128 = bf16[8,2,7,8,128]{4,3,2,1,0:T(8,128)(2,1)} custom-call(s32[3]{0:T(128)} %pad_add_fusion.info, bf16[256,1792]{1,0:T(8,128)(2,1)} %bitcast.67, bf16[256,1792]{1,0:T(8,128)(2,1)} %bitcast.64), custom_call_target="tpu_custom_call" | custom-call | tf_op jit(solution)/shard_map/pallas_call | solution.py:33
  31.1 3.5 %all-to-all-start.2 = ((bf16[16,56,128]{2,1,0:T(8,128)(2,1)}), bf16[16,56,128]{2,1,0:T(8,128)(2,1)S(1)}, u32[]{:S(2)}, u32[]{:S(2)}) async-start(bf16[16,56,128]{2,1,0:T(8,128)(2,1)} %bitcast.71), calls=%async_computation.2 | async-start | bytes 458752 | tf_op jit(solution)/shard_map/all_to_all | solution.py:25
  34.9 11.9 %all-to-all-done.2 = bf16[16,56,128]{2,1,0:T(8,128)(2,1)S(1)} async-done(((bf16[16,56,128]{2,1,0:T(8,128)(2,1)}), bf16[16,56,128]{2,1,0:T(8,128)(2,1)S(1)}, u32[]{:S(2)}, u32[]{:S(2)}) %all-to-all-start.2) | async-done | bytes 229408 | tf_op jit(solution)/shard_map/all_to_all | solution.py:25
  46.8 1.2 broadcast_in_dim.67
  48.0 5.8 %all-to-all-start.1 = ((bf16[16,256,128]{2,1,0:T(8,128)(2,1)}), bf16[16,256,128]{2,1,0:T(8,128)(2,1)S(1)}, u32[]{:S(2)}, u32[]{:S(2)}) async-start(bf16[16,256,128]{2,1,0:T(8,128)(2,1)} %bitcast.7), calls=%async_computation.1 | async-start | bytes 2097152 | tf_op jit(solution)/shard_map/all_to_all | solution.py:25
  54.1 0.8 add.350.dest_ref
  54.8 1.9 %shard_map.129 = bf16[256,128]{1,0:T(8,128)(2,1)} custom-call(s32[1,896]{1,0:T(1,128)} %add.350.dest_ref, bf16[896,128]{1,0:T(8,128)(2,1)} %bitcast.72), custom_call_target="tpu_custom_call" | custom-call | tf_op jit(solution)/shard_map/pallas_call | solution.py:33
  56.7 10.9 %all-to-all-done.1.kv_ref = bf16[16,256,128]{2,1,0:T(8,128)(2,1)S(1)} async-done(((bf16[16,256,128]{2,1,0:T(8,128)(2,1)}), bf16[16,256,128]{2,1,0:T(8,128)(2,1)S(1)}, u32[]{:S(2)}, u32[]{:S(2)}) %all-to-all-start.1) | async-done | bytes 1048608 | tf_op jit(solution)/shard_map/all_to_all | solution.py:25
  67.6 1.8 %broadcast_in_dim.68 = bf16[8,256,128]{2,1,0:T(8,128)(2,1)} broadcast(bf16[256,128]{1,0:T(8,128)(2,1)} %shard_map.129), dimensions={1,2} | broadcast | bytes 589824 | tf_op jit(solution)/shard_map/broadcast_in_dim | solution.py:263
  69.3 3.5 %all-to-all-start.3 = ((bf16[8,256,128]{2,1,0:T(8,128)(2,1)}), bf16[8,256,128]{2,1,0:T(8,128)(2,1)S(1)}, u32[]{:S(2)}, u32[]{:S(2)}) async-start(bf16[8,256,128]{2,1,0:T(8,128)(2,1)} %broadcast_in_dim.68), calls=%async_computation.3 | async-start | bytes 1048576 | tf_op jit(solution)/shard_map/all_to_all | solution.py:25
  73.2 0.7 convolution_bitcast_fusion
  74.0 0.6 copy.81
  74.6 12.3 %all-to-all-done.3.rows_ref = bf16[8,256,128]{2,1,0:T(8,128)(2,1)S(1)} async-done(((bf16[8,256,128]{2,1,0:T(8,128)(2,1)}), bf16[8,256,128]{2,1,0:T(8,128)(2,1)S(1)}, u32[]{:S(2)}, u32[]{:S(2)}) %all-to-all-start.3) | async-done | bytes 524320 | tf_op jit(solution)/shard_map/all_to_all | solution.py:25
  86.9 0.8 copy-done.2
  87.7 13.0 %shard_map.130 = (bf16[16,256,128]{2,1,0:T(8,128)(2,1)}, bf16[1024,128]{1,0:T(8,128)(2,1)}) custom-call(bf16[16,256,128]{2,1,0:T(8,128)(2,1)} %copy-done, bf16[8,256,128]{2,1,0:T(8,128)(2,1)} %copy-done.2, f32[2,1024]{1,0:T(2,128)} %bitcast.87), custom_call_target="tpu_custom_call" | custom-call | tf_op jit(solution)/shard_map/pallas_call | solution.py:112
  100.7 3.6 %all-to-all-start.4 = ((bf16[8,128,128]{2,1,0:T(8,128)(2,1)}), bf16[8,128,128]{2,1,0:T(8,128)(2,1)S(1)}, u32[]{:S(2)}, u32[]{:S(2)}) async-start(bf16[8,128,128]{2,1,0:T(8,128)(2,1)} %bitcast.78), calls=%async_computation.4 | async-start | bytes 524288 | tf_op jit(solution)/shard_map/all_to_all | solution.py:25
  104.3 0.7 select_n.236.dest_ref
  105.0 9.6 %all-to-all-done.4.parts_ref = bf16[8,128,128]{2,1,0:T(8,128)(2,1)S(1)} async-done(((bf16[8,128,128]{2,1,0:T(8,128)(2,1)}), bf16[8,128,128]{2,1,0:T(8,128)(2,1)S(1)}, u32[]{:S(2)}, u32[]{:S(2)}) %all-to-all-start.4) | async-done | bytes 262176 | tf_op jit(solution)/shard_map/all_to_all | solution.py:25
  114.6 0.7 copy-done.4
  115.3 1.8 %shard_map.131 = bf16[512,128]{1,0:T(8,128)(2,1)} custom-call(s32[1,512]{1,0:T(1,128)} %select_n.236.dest_ref, bf16[8,128,128]{2,1,0:T(8,128)(2,1)} %copy-done.4), custom_call_target="tpu_custom_call" | custom-call | tf_op jit(solution)/shard_map/pallas_call | solution.py:33
  117.2 3.5 %all-to-all-start.5 = ((bf16[16,32,128]{2,1,0:T(8,128)(2,1)}), bf16[16,32,128]{2,1,0:T(8,128)(2,1)S(1)}, u32[]{:S(2)}, u32[]{:S(2)}) async-start(bf16[16,32,128]{2,1,0:T(8,128)(2,1)} %bitcast.73), calls=%async_computation.5 | async-start | bytes 262144 | tf_op jit(solution)/shard_map/all_to_all | solution.py:25
  120.7 11.2 %all-to-all-done.5 = bf16[16,32,128]{2,1,0:T(8,128)(2,1)S(1)} async-done(((bf16[16,32,128]{2,1,0:T(8,128)(2,1)}), bf16[16,32,128]{2,1,0:T(8,128)(2,1)S(1)}, u32[]{:S(2)}, u32[]{:S(2)}) %all-to-all-start.5) | async-done | bytes 131104 | tf_op jit(solution)/shard_map/all_to_all | solution.py:25
  131.9 0.8 broadcast_in_dim.107
  132.7 4.6 %all-to-all-start.7 = ((bf16[8,32,512]{2,1,0:T(8,128)(2,1)}), bf16[8,32,512]{2,1,0:T(8,128)(2,1)S(1)}, u32[]{:S(2)}, u32[]{:S(2)}) async-start(bf16[8,32,512]{2,1,0:T(8,128)(2,1)} %broadcast_in_dim.107), calls=%async_computation.7 | async-start | bytes 524288 | tf_op jit(solution)/shard_map/all_to_all | solution.py:25
  137.3 1.3 compare_select_fusion.4.dest_ref
  138.5 1.8 %shard_map.132 = bf16[448,128]{1,0:T(8,128)(2,1)} custom-call(s32[1,512]{1,0:T(1,128)} %compare_select_fusion.4.dest_ref, bf16[512,128]{1,0:T(8,128)(2,1)} %bitcast.74), custom_call_target="tpu_custom_call" | custom-call | tf_op jit(solution)/shard_map/pallas_call | solution.py:33
  140.4 3.0 %all-to-all-done.7.kv_ref = bf16[8,32,512]{2,1,0:T(8,128)(2,1)S(1)} async-done(((bf16[8,32,512]{2,1,0:T(8,128)(2,1)}), bf16[8,32,512]{2,1,0:T(8,128)(2,1)S(1)}, u32[]{:S(2)}, u32[]{:S(2)}) %all-to-all-start.7) | async-done | bytes 262176 | tf_op jit(solution)/shard_map/all_to_all | solution.py:25
  143.4 9.4 %all_to_all.53 = bf16[8,56,128]{2,1,0:T(8,128)(2,1)S(1)} all-to-all(bf16[8,56,128]{2,1,0:T(8,128)(2,1)} %bitcast.77), channel_id=1, replica_groups=mesh['sample_0'=8,'sample_1'=2,'span'=8,'kvhead'=2] {'span'}, dimensions={0} | all-to-all | bytes 229376 | tf_op jit(solution)/shard_map/all_to_all | solution.py:25
  152.8 4.6 %all-to-all-start.8 = ((bf16[16,256,128]{2,1,0:T(8,128)(2,1)}), bf16[16,256,128]{2,1,0:T(8,128)(2,1)S(1)}, u32[]{:S(2)}, u32[]{:S(2)}) async-start(bf16[16,256,128]{2,1,0:T(8,128)(2,1)} %get-tuple-element.14), calls=%async_computation.8 | async-start | bytes 2097152 | tf_op jit(solution)/shard_map/all_to_all | solution.py:25
  157.4 0.6 copy.80
  158.0 0.7 copy.71.col_delta_ref
  158.8 0.7 copy.66
  159.5 0.6 pad_add_fusion.1.info
  160.1 6.5 %shard_map.133 = (bf16[32,256]{1,0:T(8,128)(2,1)}, bf16[32,256]{1,0:T(8,128)(2,1)}, f32[32,1792]{1,0:T(8,128)}) custom-call(s32[2]{0:T(128)} %pad_add_fusion.1.info, bf16[256,1792]{1,0:T(8,128)(2,1)} %bitcast.68, bf16[256,1792]{1,0:T(8,128)(2,1)} %bitcast.65, f32[14,256]{1,0:T(8,128)} %bitcast.86, f32[14,256]{1,0:T(8,128)} %bitcast.82, f32[32,14]{1,0:T(8,128)} %bitcast.85, ...), custom_call_target="tpu_custom_call" | custom-call | tf_op jit(solution)/shard_map/pallas_call | solution.py:33
  166.6 1.6 fusion.6
  168.2 1.3 all-to-all-done.8
  169.6 1.0 copy-done.1
  170.6 2.0 %shard_map.134 = (bf16[128,256]{1,0:T(8,128)(2,1)}, bf16[128,256]{1,0:T(8,128)(2,1)}) custom-call(bf16[2,8,256,128]{3,2,1,0:T(8,128)(2,1)} %bitcast.66), custom_call_target="tpu_custom_call" | custom-call | tf_op jit(solution)/shard_map/pallas_call | solution.py:33
  (67 shorter events, 2.2 us)
Async XLA Ops:
  0.6 2.2 %copy-start.5 = (bf16[1,256,1792]{2,1,0:T(8,128)(2,1)S(1)}, bf16[1,256,1792]{2,1,0:T(8,128)(2,1)}, u32[]{:S(2)}) copy-start(bf16[1,256,1792]{2,1,0:T(8,128)(2,1)} %param.10) | copy-start | bytes 2752516
  3.4 0.7 copy-start.10
  3.7 154.2 %copy-start.9 = (f32[256,14]{0,1:T(8,128)}, f32[256,14]{0,1:T(8,128)S(1)}, u32[]{:S(2)}) copy-start(f32[256,14]{0,1:T(8,128)S(1)} %fusion) | copy-start | bytes 43012
  5.6 20.6 %all-to-all-start = ((f32[16,1,512]{2,1,0:T(1,128)}), f32[16,1,512]{2,1,0:T(1,128)S(1)}, u32[]{:S(2)}, u32[]{:S(2)}) async-start(f32[16,1,512]{2,1,0:T(1,128)} %all_to_all.43), calls=%async_computation | async-start | bytes 65536 | tf_op jit(solution)/shard_map/all_to_all | solution.py:25
  28.4 6.2 %copy-start.11 = (bf16[128,256]{1,0:T(8,128)(2,1)S(1)}, bf16[128,256]{1,0:T(8,128)(2,1)}, u32[]{:S(2)}) copy-start(bf16[128,256]{1,0:T(8,128)(2,1)} %param.14) | copy-start | bytes 196612
  28.4 6.2 %copy-start.12 = (bf16[128,256]{1,0:T(8,128)(2,1)S(1)}, bf16[128,256]{1,0:T(8,128)(2,1)}, u32[]{:S(2)}) copy-start(bf16[128,256]{1,0:T(8,128)(2,1)} %param.15) | copy-start | bytes 196612
  31.1 15.8 %all-to-all-start.2 = ((bf16[16,56,128]{2,1,0:T(8,128)(2,1)}), bf16[16,56,128]{2,1,0:T(8,128)(2,1)S(1)}, u32[]{:S(2)}, u32[]{:S(2)}) async-start(bf16[16,56,128]{2,1,0:T(8,128)(2,1)} %bitcast.71), calls=%async_computation.2 | async-start | bytes 458752 | tf_op jit(solution)/shard_map/all_to_all | solution.py:25
  46.8 1.2 copy-start.6
  48.0 19.6 %all-to-all-start.1 = ((bf16[16,256,128]{2,1,0:T(8,128)(2,1)}), bf16[16,256,128]{2,1,0:T(8,128)(2,1)S(1)}, u32[]{:S(2)}, u32[]{:S(2)}) async-start(bf16[16,256,128]{2,1,0:T(8,128)(2,1)} %bitcast.7), calls=%async_computation.1 | async-start | bytes 2097152 | tf_op jit(solution)/shard_map/all_to_all | solution.py:25
  67.6 5.7 %copy-start = (bf16[16,256,128]{2,1,0:T(8,128)(2,1)}, bf16[16,256,128]{2,1,0:T(8,128)(2,1)S(1)}, u32[]{:S(2)}) copy-start(bf16[16,256,128]{2,1,0:T(8,128)(2,1)S(1)} %all-to-all-done.1.kv_ref) | copy-start | bytes 3145732
  69.3 17.6 %all-to-all-start.3 = ((bf16[8,256,128]{2,1,0:T(8,128)(2,1)}), bf16[8,256,128]{2,1,0:T(8,128)(2,1)S(1)}, u32[]{:S(2)}, u32[]{:S(2)}) async-start(bf16[8,256,128]{2,1,0:T(8,128)(2,1)} %broadcast_in_dim.68), calls=%async_computation.3 | async-start | bytes 1048576 | tf_op jit(solution)/shard_map/all_to_all | solution.py:25
  86.9 0.8 copy-start.2
  100.7 20.0 %copy-start.13 = (bf16[1,32,256]{2,1,0:T(8,128)(2,1)S(1)}, bf16[1,32,256]{2,1,0:T(8,128)(2,1)}, u32[]{:S(2)}) copy-start(bf16[1,32,256]{2,1,0:T(8,128)(2,1)} %param.17) | copy-start | bytes 49156
  100.7 20.0 %copy-start.14 = (bf16[1,32,256]{2,1,0:T(8,128)(2,1)S(1)}, bf16[1,32,256]{2,1,0:T(8,128)(2,1)}, u32[]{:S(2)}) copy-start(bf16[1,32,256]{2,1,0:T(8,128)(2,1)} %param.16) | copy-start | bytes 49156
  100.7 13.9 %all-to-all-start.4 = ((bf16[8,128,128]{2,1,0:T(8,128)(2,1)}), bf16[8,128,128]{2,1,0:T(8,128)(2,1)S(1)}, u32[]{:S(2)}, u32[]{:S(2)}) async-start(bf16[8,128,128]{2,1,0:T(8,128)(2,1)} %bitcast.78), calls=%async_computation.4 | async-start | bytes 524288 | tf_op jit(solution)/shard_map/all_to_all | solution.py:25
  114.6 0.7 copy-start.4
  117.2 14.7 %all-to-all-start.5 = ((bf16[16,32,128]{2,1,0:T(8,128)(2,1)}), bf16[16,32,128]{2,1,0:T(8,128)(2,1)S(1)}, u32[]{:S(2)}, u32[]{:S(2)}) async-start(bf16[16,32,128]{2,1,0:T(8,128)(2,1)} %bitcast.73), calls=%async_computation.5 | async-start | bytes 262144 | tf_op jit(solution)/shard_map/all_to_all | solution.py:25
  120.7 32.1 %copy-start.8 = (bf16[32,512]{1,0:T(8,128)(2,1)}, bf16[32,512]{1,0:T(8,128)(2,1)S(1)}, u32[]{:S(2)}) copy-start(bf16[32,512]{1,0:T(8,128)(2,1)S(1)} %pad_maximum_fusion.1.own_ref) | copy-start | bytes 98308
  131.9 6.6 %copy-start.7 = (bf16[16,32,128]{2,1,0:T(8,128)(2,1)}, bf16[16,32,128]{2,1,0:T(8,128)(2,1)S(1)}, u32[]{:S(2)}) copy-start(bf16[16,32,128]{2,1,0:T(8,128)(2,1)S(1)} %all-to-all-done.5) | copy-start | bytes 393220
  132.7 10.7 %all-to-all-start.7 = ((bf16[8,32,512]{2,1,0:T(8,128)(2,1)}), bf16[8,32,512]{2,1,0:T(8,128)(2,1)S(1)}, u32[]{:S(2)}, u32[]{:S(2)}) async-start(bf16[8,32,512]{2,1,0:T(8,128)(2,1)} %broadcast_in_dim.107), calls=%async_computation.7 | async-start | bytes 524288 | tf_op jit(solution)/shard_map/all_to_all | solution.py:25
  143.4 9.4 %copy-start.3 = (bf16[8,32,512]{2,1,0:T(8,128)(2,1)}, bf16[8,32,512]{2,1,0:T(8,128)(2,1)S(1)}, u32[]{:S(2)}) copy-start(bf16[8,32,512]{2,1,0:T(8,128)(2,1)S(1)} %all-to-all-done.7.kv_ref) | copy-start | bytes 786436
  152.8 16.8 %all-to-all-start.8 = ((bf16[16,256,128]{2,1,0:T(8,128)(2,1)}), bf16[16,256,128]{2,1,0:T(8,128)(2,1)S(1)}, u32[]{:S(2)}, u32[]{:S(2)}) async-start(bf16[16,256,128]{2,1,0:T(8,128)(2,1)} %get-tuple-element.14), calls=%async_computation.8 | async-start | bytes 2097152 | tf_op jit(solution)/shard_map/all_to_all | solution.py:25
  169.6 1.0 copy-start.1

commit v2 on v1

v2 whole, which is shorter than its diff:
```python
import math

import jax
import jax.numpy as jnp
from jax import lax
from jax.experimental import pallas as pl
from jax.experimental.pallas import tpu as pltpu
from jax.sharding import Mesh
from jax.sharding import PartitionSpec as P

HEAD_WIDTH = 128
SAMPLE = ("sample_0", "sample_1")
PLANE = ("sample_1", "span")
SAMPLE_SPAN = ("sample_0", "sample_1", "span")
GROUP = 7
CLASSES = 8
SLOTS = 24
LIVE = 144
STATS = GROUP * HEAD_WIDTH
INTERPRET = False
BF16 = jnp.bfloat16
F32 = jnp.float32
SCALE = 1.0 / math.sqrt(HEAD_WIDTH)
EXACT = lax.Precision.HIGHEST


def exchange(tiles, axes):
    return lax.all_to_all(tiles, axes, split_axis=0, concat_axis=0, tiled=True)


def dot(a, b, ca, cb):
    return lax.dot_general(a, b, (((ca,), (cb,)), ((), ())), preferred_element_type=F32)


def call(body, out_shape, *args, **kw):
    return pl.pallas_call(body, out_shape=out_shape, interpret=INTERPRET, **kw)(*args)


def stat_lanes(shape):
    lane = lax.broadcasted_iota(jnp.int32, shape, 1)
    group = jnp.zeros(shape, jnp.int32)
    for edge in range(GROUP, 6 * GROUP, GROUP):
        group = group + jnp.where(lane >= edge, 1, 0)
    piece = jnp.where(group >= 3, group - 3, group)
    return lane, lane - GROUP * group, piece


def pick_kernel(info, q_ref, o_ref, g_ref, norm_ref, out_ref):
    p, turn, live = info[0], info[1], info[2]
    row = lax.broadcasted_iota(jnp.int32, (64, 256), 0)
    i = lax.broadcasted_iota(jnp.int32, (64, 256), 1)
    hit = (i % 8 == p) & (i < live) & ((turn + i // 8) % 8 == row // 8) & (i // 64 == row % 4)
    pick_q = jnp.where(hit & (row % 8 < 4), 1.0, 0.0)
    pick_g = jnp.where(hit & (row % 8 >= 4), 1.0, 0.0).astype(BF16)
    lane, head_of, piece = stat_lanes((64, HEAD_WIDTH))
    pick_q_low = pick_q.astype(BF16)
    for half in range(2):
        lanes = slice(half * STATS, (half + 1) * STATS)
        both = dot(pick_q_low, q_ref[:, lanes], 1, 0) + dot(pick_g, g_ref[:, lanes], 1, 0)
        out_ref[:, half, :, 0:STATS] = both.reshape(8, 8, STATS).astype(BF16)
        product = dot(pick_q_low, o_ref[:, lanes], 1, 0) * dot(pick_q_low, g_ref[:, lanes], 1, 0)
        stat = jnp.zeros((64, HEAD_WIDTH), F32)
        for inner in range(GROUP):
            mine = head_of == inner
            part = product[:, inner * HEAD_WIDTH : (inner + 1) * HEAD_WIDTH]
            delta = jnp.sum(part, axis=1, keepdims=True)
            norm = norm_ref[half * GROUP + inner : half * GROUP + inner + 1, :]
            norm = jnp.sum(pick_q * norm, axis=1, keepdims=True) * math.sqrt(HEAD_WIDTH)
            stat = jnp.where(mine & (lane < 3 * GROUP), norm, stat)
            stat = jnp.where(mine & (lane >= 3 * GROUP) & (lane < 6 * GROUP), delta, stat)
        high = stat.astype(BF16).astype(F32)
        middle = (stat - high).astype(BF16).astype(F32)
        low = stat - high - middle
        stat = jnp.where(piece == 0, high, jnp.where(piece == 1, middle, low))
        stat = jnp.where(lane == 6 * GROUP, live.astype(F32), stat)
        out_ref[:, half, :, STATS:] = stat.reshape(8, 8, HEAD_WIDTH).astype(BF16)


def compact_kernel(dest_ref, rows_ref, out_ref):
    total = out_ref.shape[1]
    dest = dest_ref[0:1, :]
    hit = lax.broadcasted_iota(jnp.int32, (total, dest.shape[1]), 0) == dest
    rows = rows_ref[...].reshape(dest.shape[1], -1)
    rows = dot(jnp.where(hit, 1.0, 0.0).astype(BF16), rows, 1, 0).astype(BF16)
    for copy in range(out_ref.shape[0]):
        out_ref[copy] = rows


def prompt_kernel(
    in_slot_ref, out_slot_ref, kv_ref, rows_ref, kvg_ref, gq_ref, q_scr, g_scr, acc_ref, back_ref
):
    step = pl.program_id(0)

    @pl.when(step == 0)
    def _():
        acc_ref[...] = jnp.zeros_like(acc_ref)
        slot = in_slot_ref[0:1, :]
        hit = lax.broadcasted_iota(jnp.int32, (2 * LIVE, slot.shape[1]), 0) == slot
        pick = jnp.where(hit, 1.0, 0.0).astype(BF16)
        rows = dot(pick, rows_ref[...].reshape(slot.shape[1], -1), 1, 0).astype(BF16)
        lane, head_of, _ = stat_lanes((LIVE, HEAD_WIDTH))
        stats = rows[0:LIVE, STATS:]
        zero = jnp.zeros((), BF16)
        for head in range(GROUP):
            place = slice(head * LIVE, (head + 1) * LIVE)
            lanes = slice(head * HEAD_WIDTH, (head + 1) * HEAD_WIDTH)
            mine = head_of == head
            q_scr[place, 0:HEAD_WIDTH] = rows[0:LIVE, lanes]
            q_scr[place, HEAD_WIDTH:] = jnp.where(mine & (lane < 3 * GROUP), stats, zero)
            g_scr[place, 0:HEAD_WIDTH] = rows[LIVE:, lanes]
            g_scr[place, HEAD_WIDTH:] = jnp.where(
                mine & (lane >= 3 * GROUP) & (lane < 6 * GROUP), stats, zero
            )
        q_scr[GROUP * LIVE :, :] = jnp.zeros((1024 - GROUP * LIVE, 2 * HEAD_WIDTH), BF16)
        g_scr[GROUP * LIVE :, :] = jnp.zeros((1024 - GROUP * LIVE, 2 * HEAD_WIDTH), BF16)

    keys = kv_ref[:, 0:128, :].reshape(-1, HEAD_WIDTH)
    values = kv_ref[:, 128:256, :].reshape(-1, HEAD_WIDTH)
    lane = lax.broadcasted_iota(jnp.int32, keys.shape, 1)
    minus = jnp.where(lane < 6 * GROUP, -1.0, 0.0).astype(BF16)
    wide_keys = jnp.concatenate([keys, minus], axis=1)
    wide_values = jnp.concatenate([values, minus], axis=1)
    gk = jnp.zeros(keys.shape, F32)
    gv = jnp.zeros(keys.shape, F32)
    for part in range(4):
        rows = slice(256 * part, 256 * part + 256)
        prob = jnp.exp(dot(wide_keys, q_scr[rows, :], 1, 1) * SCALE)
        sgrad = (prob * dot(wide_values, g_scr[rows, :], 1, 1)).astype(BF16)
        gv = gv + dot(prob.astype(BF16), g_scr[rows, 0:HEAD_WIDTH], 1, 0)
        gk = gk + dot(sgrad, q_scr[rows, 0:HEAD_WIDTH], 1, 0)
        acc_ref[rows, :] += dot(sgrad, keys, 0, 0)
    kvg_ref[:, 0:128, :] = (gk * SCALE).astype(BF16).reshape(-1, 128, HEAD_WIDTH)
    kvg_ref[:, 128:256, :] = gv.astype(BF16).reshape(-1, 128, HEAD_WIDTH)

    @pl.when(step == pl.num_programs(0) - 1)
    def _():
        back_ref[...] = jnp.zeros_like(back_ref)
        for head in range(GROUP):
            lanes = slice(head % 4 * HEAD_WIDTH, (head % 4 + 1) * HEAD_WIDTH)
            part = (acc_ref[head * LIVE : (head + 1) * LIVE, :] * SCALE).astype(BF16)
            back_ref[head // 4 * LIVE : (head // 4 + 1) * LIVE, lanes] = part
        slot = out_slot_ref[0:1, :]
        hit = lax.broadcasted_iota(jnp.int32, (2 * LIVE, slot.shape[1]), 0) == slot
        pick = jnp.where(hit, 1.0, 0.0).astype(BF16)
        gq_ref[...] = dot(pick, back_ref[...], 0, 0).reshape(gq_ref.shape).astype(BF16)


def prompt_terms(in_slot, out_slot, kv, rows):
    sources = kv.shape[0]
    per = 2
    block = pl.BlockSpec((per, 256, HEAD_WIDTH), lambda k: (k, 0, 0))
    return pl.pallas_call(
        prompt_kernel,
        grid=(sources // per,),
        in_specs=[
            pl.BlockSpec(in_slot.shape, lambda k: (0, 0)),
            pl.BlockSpec(out_slot.shape, lambda k: (0, 0)),
            block,
            pl.BlockSpec(rows.shape, lambda k: (0, 0, 0)),
        ],
        out_specs=[block, pl.BlockSpec((128, 8, 512), lambda k: (0, 0, 0))],
        out_shape=[
            jax.ShapeDtypeStruct(kv.shape, BF16),
            jax.ShapeDtypeStruct((128, 8, 512), BF16),
        ],
        scratch_shapes=[
            pltpu.VMEM((1024, 2 * HEAD_WIDTH), BF16),
            pltpu.VMEM((1024, 2 * HEAD_WIDTH), BF16),
            pltpu.VMEM((1024, HEAD_WIDTH), F32),
            pltpu.VMEM((2 * LIVE, 512), BF16),
        ],
        interpret=INTERPRET,
    )(in_slot, out_slot, kv, rows)


def final_kernel(parts_ref, own_ref, out_ref, sum_ref):
    for half in range(2):
        for p in range(CLASSES):
            total = parts_ref[half * 8 + p].astype(F32)
            for z in range(1, 8):
                total = total + parts_ref[z * 16 + half * 8 + p].astype(F32)
            for head in range(GROUP):
                rows = slice(head // 4 * 4, head // 4 * 4 + 4)
                part = total[rows, head % 4 * HEAD_WIDTH : (head % 4 + 1) * HEAD_WIDTH]
                first = (half * GROUP + head) * 32 + p
                sum_ref[pl.ds(first, 4, stride=8), :] = part
    for head in range(2 * GROUP):
        lanes = slice(head * HEAD_WIDTH, (head + 1) * HEAD_WIDTH)
        out_ref[:, lanes] = (sum_ref[head * 32 : head * 32 + 32, :] + own_ref[:, lanes]).astype(BF16)


def key_sum_kernel(parts_ref, k_ref, v_ref):
    for head in range(2):
        total = parts_ref[head, 0].astype(F32)
        for k in range(1, parts_ref.shape[1]):
            total = total + parts_ref[head, k].astype(F32)
        lanes = slice(head * HEAD_WIDTH, (head + 1) * HEAD_WIDTH)
        k_ref[:, lanes] = total[0:128].astype(BF16)
        v_ref[:, lanes] = total[128:256].astype(BF16)


def self_kernel(
    info, q_ref, g_ref, norm_ref, delta_ref, col_norm_ref, col_delta_ref, own_ref, kv_ref,
    gk_ref, gv_ref, gq_ref,
):
    p, live = info[0], info[1]
    rows_total = q_ref.shape[0]
    i_row = lax.broadcasted_iota(jnp.int32, (32, rows_total), 1)
    j_row = lax.broadcasted_iota(jnp.int32, (32, rows_total), 0) + p * 32
    live_row = lax.broadcasted_iota(jnp.int32, (rows_total, HEAD_WIDTH), 0) < live
    live_own = lax.broadcasted_iota(jnp.int32, (32, HEAD_WIDTH), 0) + p * 32 < live
    zero = jnp.zeros((), BF16)
    for kv in range(2):
        key_lanes = slice(kv * HEAD_WIDTH, (kv + 1) * HEAD_WIDTH)
        value_lanes = slice((kv + 2) * HEAD_WIDTH, (kv + 3) * HEAD_WIDTH)
        keys, values = own_ref[:, key_lanes], own_ref[:, value_lanes]
        all_keys = kv_ref[:, :, key_lanes].reshape(rows_total, HEAD_WIDTH)
        all_values = kv_ref[:, :, value_lanes].reshape(rows_total, HEAD_WIDTH)
        gk = jnp.zeros((32, HEAD_WIDTH), F32)
        gv = jnp.zeros((32, HEAD_WIDTH), F32)
        for inner in range(GROUP):
            head = kv * GROUP + inner
            lanes = slice(head * HEAD_WIDTH, (head + 1) * HEAD_WIDTH)
            q = q_ref[:, lanes]
            g = jnp.where(live_row, g_ref[:, lanes], zero)
            prob = jnp.exp(dot(keys, q, 1, 1) * SCALE - norm_ref[head : head + 1, :])
            prob = jnp.where(j_row <= i_row, prob, 0.0)
            sgrad = prob * (dot(values, g, 1, 1) - delta_ref[head : head + 1, :])
            gv = gv + dot(prob.astype(BF16), g, 1, 0)
            gk = gk + dot(sgrad.astype(BF16), q, 1, 0)
            q_own = q_ref[pl.ds(pl.multiple_of(p * 32, 32), 32), lanes]
            g_own = g_ref[pl.ds(pl.multiple_of(p * 32, 32), 32), lanes]
            g_own = jnp.where(live_own, g_own, zero)
            prob = jnp.exp(dot(q_own, all_keys, 1, 1) * SCALE - col_norm_ref[:, head : head + 1])
            i_own = lax.broadcasted_iota(jnp.int32, prob.shape, 0) + p * 32
            prob = jnp.where(lax.broadcasted_iota(jnp.int32, prob.shape, 1) <= i_own, prob, 0.0)
            sgrad = prob * (dot(g_own, all_values, 1, 1) - col_delta_ref[:, head : head + 1])
            gq_ref[:, lanes] = dot(sgrad.astype(BF16), all_keys, 1, 0) * SCALE
        gk_ref[:, key_lanes] = (gk * SCALE).astype(BF16)
        gv_ref[:, key_lanes] = gv.astype(BF16)


def shards(
    queries,
    outputs,
    grad_out,
    log_norms,
    lengths,
    prompt_key_rows,
    prompt_value_rows,
    slice_key_rows,
    slice_value_rows,
):
    z = lax.axis_index("sample_0")
    half = lax.axis_index("sample_1")
    p = lax.axis_index("span")
    sample = 2 * z + half
    spans = lax.axis_size("span")
    slice_rows = queries.shape[1]
    heads = queries.shape[2] // HEAD_WIDTH
    class_rows = slice_rows // CLASSES
    q, o, g = queries[0], outputs[0], grad_out[0]
    norms = log_norms[0]
    live = lengths[0]
    smem, vmem = pl.BlockSpec(memory_space=pltpu.SMEM), pl.BlockSpec(memory_space=pltpu.VMEM)

    kv_heads = jnp.concatenate(
        [
            prompt_key_rows.reshape(-1, 2, HEAD_WIDTH).transpose(1, 0, 2),
            prompt_value_rows.reshape(-1, 2, HEAD_WIDTH).transpose(1, 0, 2),
        ],
        axis=1,
    )
    kv_send = jnp.broadcast_to(kv_heads[:, None], (2, spans, *kv_heads.shape[1:]))
    kv = exchange(kv_send.reshape(2 * spans, *kv_heads.shape[1:]), PLANE)

    picked = call(
        pick_kernel,
        jax.ShapeDtypeStruct((8, 2, 8, 1024), BF16),
        jnp.stack([p, sample % 8, live]),
        q,
        o,
        g,
        norms,
        in_specs=[smem] + [vmem] * 4,
    )
    arrived = exchange(picked.reshape(16, 8, 1024), SAMPLE)

    all_lengths = arrived[:, 0, STATS + 6 * GROUP].astype(jnp.int32)
    live_of = jnp.clip((all_lengths - p + CLASSES - 1) // CLASSES, 0, class_rows)
    every_sample = jnp.arange(16)
    first = (jnp.arange(8)[None, :] - every_sample[:, None]) % 8
    held = jnp.clip((live_of[:, None] - first + 7) // 8, 0, 4)
    earlier = (every_sample[None, :] < every_sample[:, None])[:, :, None]
    before = jnp.sum(jnp.where(earlier, held[None], 0), axis=1)
    total = jnp.sum(held, axis=0)
    base = jnp.sum(jnp.where(jnp.arange(8)[None, :] < jnp.arange(8)[:, None], total[None], 0), axis=1)
    mine = jnp.arange(8)[None, :] == z
    own_held = jnp.sum(jnp.where(mine, held, 0), axis=1)
    own_before = jnp.sum(jnp.where(mine, before, 0), axis=1)
    step4 = jnp.arange(4)[None, :]
    compact_slot = jnp.where(step4 < own_held[:, None], own_before[:, None] + step4, -SLOTS)
    compact_dest = compact_slot[:, None, :] + SLOTS * jnp.arange(2)[None, :, None]
    compact_dest = jnp.where(compact_slot[:, None, :] < 0, -1, compact_dest)
    compact = call(
        compact_kernel,
        jax.ShapeDtypeStruct((8, 2 * SLOTS, 1024), BF16),
        compact_dest.reshape(1, 128),
        arrived,
    )
    rows = exchange(compact, "sample_0")
    step = jnp.arange(SLOTS)[None, :]
    in_slot = base[:, None] + step
    in_slot = in_slot[:, None, :] + LIVE * jnp.arange(2)[None, :, None]
    in_slot = jnp.where((step < total[:, None])[:, None, :], in_slot, -1).reshape(1, 16 * SLOTS)
    k = jnp.arange(class_rows)
    holder = (k[None, :] + every_sample[:, None]) % 8
    chosen = holder[:, :, None] == jnp.arange(8)[None, None, :]
    slot_of = jnp.sum(jnp.where(chosen, (base[None, :] + before)[:, None, :], 0), axis=2)
    slot_of = jnp.where(k[None, :] < live_of[:, None], slot_of + k[None, :] // 8, -LIVE * 2)
    out_slot = slot_of.reshape(16, spans, 1, 4) + LIVE * jnp.arange(2)[None, None, :, None]
    out_slot = out_slot.reshape(1, 1024)

    live_rows = lax.broadcasted_iota(jnp.int32, (slice_rows, 1), 0) < live
    g_live = jnp.where(live_rows, g, jnp.zeros((), BF16))
    delta = jnp.sum(
        (g_live.astype(F32) * o.astype(F32)).reshape(slice_rows, heads, HEAD_WIDTH), axis=-1
    ).T
    own_kv = jnp.concatenate([slice_key_rows[0], slice_value_rows[0]], axis=1)
    slice_kv = exchange(jnp.broadcast_to(own_kv[None], (spans, *own_kv.shape)), "span")
    own_rows = slice_rows // spans
    col_norms = lax.dynamic_slice_in_dim(norms, p * own_rows, own_rows, 1).T
    col_delta = lax.dynamic_slice_in_dim(delta, p * own_rows, own_rows, 1).T
    own_shape = jax.ShapeDtypeStruct((own_rows, 2 * HEAD_WIDTH), BF16)
    gk_self, gv_self, gq_self = call(
        self_kernel,
        [own_shape, own_shape, jax.ShapeDtypeStruct((own_rows, heads * HEAD_WIDTH), F32)],
        jnp.stack([p, live]),
        q,
        g,
        norms,
        delta,
        col_norms,
        col_delta,
        own_kv,
        slice_kv,
        in_specs=[smem] + [vmem] * 8,
    )

    kv_grads, gq_parts = prompt_terms(in_slot, out_slot, kv, rows)
    gq_parts = exchange(gq_parts, SAMPLE_SPAN)
    kv_parts = exchange(kv_grads, PLANE)
    prompt_shape = jax.ShapeDtypeStruct(prompt_key_rows.shape, BF16)
    gk_prompt, gv_prompt = call(
        key_sum_kernel,
        [prompt_shape, prompt_shape],
        kv_parts.reshape(2, spans, *kv_parts.shape[1:]),
    )
    grad_query = call(
        final_kernel,
        jax.ShapeDtypeStruct((own_rows, heads * HEAD_WIDTH), BF16),
        gq_parts,
        gq_self,
        scratch_shapes=[pltpu.VMEM((heads * own_rows, HEAD_WIDTH), F32)],
    )
    return grad_query[None], gk_prompt, gv_prompt, gk_self[None], gv_self[None]


def solution(mesh):
    split = Mesh(
        mesh.devices.reshape(8, 2, mesh.shape["span"], mesh.shape["kvhead"]),
        ("sample_0", "sample_1", "span", "kvhead"),
    )
    placed = (
        P(SAMPLE, None, "kvhead"),
        P(SAMPLE, None, "kvhead"),
        P(SAMPLE, None, "kvhead"),
        P(SAMPLE, "kvhead", None),
        P(SAMPLE),
        P(SAMPLE_SPAN, "kvhead"),
        P(SAMPLE_SPAN, "kvhead"),
        P(SAMPLE, "span", "kvhead"),
        P(SAMPLE, "span", "kvhead"),
    )
    return jax.shard_map(
        shards,
        mesh=split,
        in_specs=placed,
        out_specs=(
            P(SAMPLE, "span", "kvhead"),
            P(SAMPLE_SPAN, "kvhead"),
            P(SAMPLE_SPAN, "kvhead"),
            P(SAMPLE, "span", "kvhead"),
            P(SAMPLE, "span", "kvhead"),
        ),
        check_vma=False,
    )
```

time: 174 us -> 159 us (0.914)
  waiting for transfers between devices: 70.5 us -> 57.2 us
  blocking collectives: 9.41 us -> 21.1 us
  starting transfers between devices: 39.3 us -> 31.3 us
  local copies, waits for them, and re-layouts: 14.7 us -> 10.8 us
  other arithmetic: 6.69 us -> 4.91 us
    all_to_all x8 -> x5, waiting for transfers between devices: 70.5 us -> 57.2 us  [exchange(): return lax.all_to_all(tiles, axes, split_axis=0, concat_axis=0, tiled=True)]
    all_to_all x1, blocking collectives: 9.41 us -> 21.1 us  [exchange(): return lax.all_to_all(tiles, axes, split_axis=0, concat_axis=0, tiled=True)]
    all_to_all x8 -> x5, starting transfers between devices: 39.3 us -> 31.3 us  [exchange(): return lax.all_to_all(tiles, axes, split_axis=0, concat_axis=0, tiled=True)]
    pallas_call x1, Pallas kernels: 13 us -> 14.8 us  [prompt_terms(): pl.pallas_call(prompt_kernel, grid=(sources // per,), in_specs=[pl.BlockS...]
    select_n x5 -> x6, other arithmetic: 2.14 us -> 0.32 us  [the longest x1 0.08 us: shards(): jnp.where(k[None, :] < live_of[:, None], slot_of + k[None, :] // 8, -LIVE...]
    broadcast_in_dim x2 -> x0, local copies, waits for them, and re-layouts: 1.76 us -> none  [the longest x1 1.75 us: shards(): jnp.broadcast_to(compact[None], (8, 256, HEAD_WIDTH))]
    unnamed x37 -> x34, local copies, waits for them, and re-layouts: 6.64 us -> 5.63 us
    pallas_call x6 -> x5, Pallas kernels: 16.6 us -> 15.8 us  [call(): pl.pallas_call(body, out_shape=out_shape, interpret=INTERPRET, **kw)(*args)]
  transfers between devices with their start and end apart: 8 -> 5, of which waited for: 8 -> 4; matrix products, arithmetic and copies ran while one was open for 6% -> 7% of each run, Pallas kernels for 6% -> 16%
where the time goes in v2:
time: 159 us; the launch traced here: 158 us
  waiting for transfers between devices  57.2 us (36%)
  starting transfers between devices  31.3 us (20%)
  Pallas kernels  30.7 us (19%)
  blocking collectives  21.1 us (13%)
  local copies, waits for them, and re-layouts  10.8 us (7%)
  other arithmetic  4.91 us (3%)
    all_to_all x5, waiting for transfers between devices, exchange(): return lax.all_to_all(tiles, axes, split_axis=0, concat_axis=0, tiled=True)  57.2 us
    all_to_all x5, starting transfers between devices, exchange(): return lax.all_to_all(tiles, axes, split_axis=0, concat_axis=0, tiled=True)  31.3 us
    all_to_all x1, blocking collectives, exchange(): return lax.all_to_all(tiles, axes, split_axis=0, concat_axis=0, tiled=True)  21.1 us
    pallas_call x5, Pallas kernels, call(): pl.pallas_call(body, out_shape=out_shape, interpret=INTERPRET, **kw)(*args)  15.8 us
    pallas_call x1, Pallas kernels, prompt_terms(): pl.pallas_call(prompt_kernel, grid=(sources // per,), in_specs=[pl.BlockS...  14.8 us
    unnamed x34, local copies, waits for them, and re-layouts  5.63 us
  transfers between devices with their start and end apart: 5, of which 4 were waited for; matrix products, arithmetic and copies ran while one was open for 7% of the time, Pallas kernels for 16%

profile of v2, /device:TPU:8, one launch (start us, length us, event | category | flops | bytes accessed | tf_op | source)
XLA Modules:
  0.0 157.5 jit_solution(17991743275480162807)
XLA Ops:
  1.3 1.3 copy.46
  2.6 0.6 pad_add_fusion.info
  3.2 3.3 %shard_map.128 = bf16[8,2,8,1024]{3,2,1,0:T(8,128)(2,1)} custom-call(s32[3]{0:T(128)} %pad_add_fusion.info, bf16[256,1792]{1,0:T(8,128)(2,1)} %bitcast.32, bf16[256,1792]{1,0:T(8,128)(2,1)} %bitcast.31, bf16[256,1792]{1,0:T(8,128)(2,1)} %bitcast.28, f32[14,256]{1,0:T(8,128)} %bitcast.39), custom_call_target="tpu_custom_call" | custom-call | tf_op jit(solution)/shard_map/pallas_call | solution.py:36
  6.5 10.3 %all-to-all-start = ((bf16[16,8,1024]{2,1,0:T(8,128)(2,1)}), bf16[16,8,1024]{2,1,0:T(8,128)(2,1)S(1)}, u32[]{:S(2)}, u32[]{:S(2)}) async-start(bf16[16,8,1024]{2,1,0:T(8,128)(2,1)} %bitcast.36), calls=%async_computation | async-start | bytes 524288 | tf_op jit(solution)/shard_map/all_to_all | solution.py:28
  16.8 0.2 pad_maximum_fusion
  17.1 13.2 %all-to-all-done.rows_ref = bf16[16,8,1024]{2,1,0:T(8,128)(2,1)S(1)} async-done(((bf16[16,8,1024]{2,1,0:T(8,128)(2,1)}), bf16[16,8,1024]{2,1,0:T(8,128)(2,1)S(1)}, u32[]{:S(2)}, u32[]{:S(2)}) %all-to-all-start) | async-done | bytes 262176 | tf_op jit(solution)/shard_map/all_to_all | solution.py:28
  30.3 1.2 broadcast_in_dim.166
  31.4 5.8 %all-to-all-start.1 = ((bf16[16,256,128]{2,1,0:T(8,128)(2,1)}), bf16[16,256,128]{2,1,0:T(8,128)(2,1)S(1)}, u32[]{:S(2)}, u32[]{:S(2)}) async-start(bf16[16,256,128]{2,1,0:T(8,128)(2,1)} %bitcast.9), calls=%async_computation.1 | async-start | bytes 2097152 | tf_op jit(solution)/shard_map/all_to_all | solution.py:28
  37.2 0.5 fusion.13
  37.7 0.1 fusion.5
  37.9 0.4 select_reduce_fusion.1
  38.2 0.2 select_reduce_fusion.3
  38.4 0.1 broadcast_compare_fusion
  38.5 0.1 add_select_fusion.5
  38.6 0.1 add_select_fusion
  38.6 0.6 select_n.150.dest_ref
  39.3 2.1 %shard_map.129 = bf16[8,48,1024]{2,1,0:T(8,128)(2,1)} custom-call(s32[1,128]{1,0:T(1,128)} %select_n.150.dest_ref, bf16[16,8,1024]{2,1,0:T(8,128)(2,1)} %copy-done.6), custom_call_target="tpu_custom_call" | custom-call | tf_op jit(solution)/shard_map/pallas_call | solution.py:36
  41.3 10.4 %all-to-all-done.1.kv_ref = bf16[16,256,128]{2,1,0:T(8,128)(2,1)S(1)} async-done(((bf16[16,256,128]{2,1,0:T(8,128)(2,1)}), bf16[16,256,128]{2,1,0:T(8,128)(2,1)S(1)}, u32[]{:S(2)}, u32[]{:S(2)}) %all-to-all-start.1) | async-done | bytes 1048608 | tf_op jit(solution)/shard_map/all_to_all | solution.py:28
  51.8 3.7 %all-to-all-start.2 = ((bf16[8,48,1024]{2,1,0:T(8,128)(2,1)}), bf16[8,48,1024]{2,1,0:T(8,128)(2,1)S(1)}, u32[]{:S(2)}, u32[]{:S(2)}) async-start(bf16[8,48,1024]{2,1,0:T(8,128)(2,1)} %shard_map.129), calls=%async_computation.2 | async-start | bytes 1572864 | tf_op jit(solution)/shard_map/all_to_all | solution.py:28
  55.5 0.1 select_reduce_fusion.4
  55.7 0.1 select_reduce_fusion
  55.8 0.1 copy.31
  55.8 0.1 iota_compare_fusion.4
  56.0 0.1 add_select_fusion.1
  56.1 20.4 %all-to-all-done.2.rows_ref = bf16[8,48,1024]{2,1,0:T(8,128)(2,1)S(1)} async-done(((bf16[8,48,1024]{2,1,0:T(8,128)(2,1)}), bf16[8,48,1024]{2,1,0:T(8,128)(2,1)S(1)}, u32[]{:S(2)}, u32[]{:S(2)}) %all-to-all-start.2) | async-done | bytes 786464 | tf_op jit(solution)/shard_map/all_to_all | solution.py:28
  76.4 0.8 broadcast_in_dim.173
  77.2 4.8 %all-to-all-start.4 = ((bf16[8,32,512]{2,1,0:T(8,128)(2,1)}), bf16[8,32,512]{2,1,0:T(8,128)(2,1)S(1)}, u32[]{:S(2)}, u32[]{:S(2)}) async-start(bf16[8,32,512]{2,1,0:T(8,128)(2,1)} %broadcast_in_dim.173), calls=%async_computation.4 | async-start | bytes 524288 | tf_op jit(solution)/shard_map/all_to_all | solution.py:28
  82.0 0.1 add_select_fusion.6
  82.1 0.7 select_n.140.in_slot_ref
  82.7 0.1 copy.32
  82.8 0.1 broadcast_add_fusion
  83.0 0.8 add.229.out_slot_ref
  83.8 14.8 %shard_map.130 = (bf16[16,256,128]{2,1,0:T(8,128)(2,1)}, bf16[128,8,512]{2,1,0:T(8,128)(2,1)}) custom-call(s32[1,384]{1,0:T(1,128)} %select_n.140.in_slot_ref, s32[1,1024]{1,0:T(1,128)} %add.229.out_slot_ref, bf16[16,256,128]{2,1,0:T(8,128)(2,1)} %copy-done.1, bf16[8,48,1024]{2,1,0:T(8,128)(2,1)} %copy-done.5), custom_call_target="tpu_custom_call" | custom-call | tf_op jit(solution)/shard_map/pallas_call | solution.py:152
  98.6 21.1 %all_to_all.30 = bf16[16,256,128]{2,1,0:T(8,128)(2,1)} all-to-all(bf16[16,256,128]{2,1,0:T(8,128)(2,1)} %get-tuple-element.14), channel_id=1, replica_groups=mesh['sample_0'=8,'sample_1'=2,'span'=8,'kvhead'=2] {'sample_1','span'}, dimensions={0} | all-to-all | bytes 2097152 | tf_op jit(solution)/shard_map/all_to_all | solution.py:28
  119.7 6.8 %all-to-all-start.3 = ((bf16[128,8,512]{2,1,0:T(8,128)(2,1)}), bf16[128,8,512]{2,1,0:T(8,128)(2,1)S(1)}, u32[]{:S(2)}, u32[]{:S(2)}) async-start(bf16[128,8,512]{2,1,0:T(8,128)(2,1)} %get-tuple-element.12), calls=%async_computation.3 | async-start | bytes 2097152 | tf_op jit(solution)/shard_map/all_to_all | solution.py:28
  126.5 1.3 copy.37
  127.8 1.3 copy.36
  129.1 0.1 constant_dynamic-slice_fusion.1
  129.2 0.7 copy.38
  129.9 1.5 fusion
  131.4 0.1 constant_dynamic-slice_fusion
  131.5 0.7 copy.44.col_delta_ref
  132.1 0.6 pad_add_fusion.1.info
  132.8 6.5 %shard_map.131 = (bf16[32,256]{1,0:T(8,128)(2,1)}, bf16[32,256]{1,0:T(8,128)(2,1)}, f32[32,1792]{1,0:T(8,128)}) custom-call(s32[2]{0:T(128)} %pad_add_fusion.1.info, bf16[256,1792]{1,0:T(8,128)(2,1)} %bitcast.33, bf16[256,1792]{1,0:T(8,128)(2,1)} %bitcast.29, f32[14,256]{1,0:T(8,128)} %bitcast.40, f32[14,256]{1,0:T(8,128)} %bitcast.42, f32[32,14]{1,0:T(8,128)} %bitcast.43, ...), custom_call_target="tpu_custom_call" | custom-call | tf_op jit(solution)/shard_map/pallas_call | solution.py:36
  139.3 2.0 %shard_map.133 = (bf16[128,256]{1,0:T(8,128)(2,1)}, bf16[128,256]{1,0:T(8,128)(2,1)}) custom-call(bf16[2,8,256,128]{3,2,1,0:T(8,128)(2,1)} %bitcast.30), custom_call_target="tpu_custom_call" | custom-call | tf_op jit(solution)/shard_map/pallas_call | solution.py:36
  141.3 13.2 %all-to-all-done.3.parts_ref = bf16[128,8,512]{2,1,0:T(8,128)(2,1)S(1)} async-done(((bf16[128,8,512]{2,1,0:T(8,128)(2,1)}), bf16[128,8,512]{2,1,0:T(8,128)(2,1)S(1)}, u32[]{:S(2)}, u32[]{:S(2)}) %all-to-all-start.3) | async-done | bytes 1048608 | tf_op jit(solution)/shard_map/all_to_all | solution.py:28
  154.5 1.0 copy-done.2
  155.5 2.1 %shard_map.132 = bf16[32,1792]{1,0:T(8,128)(2,1)} custom-call(bf16[128,8,512]{2,1,0:T(8,128)(2,1)} %copy-done.2, f32[32,1792]{1,0:T(8,128)} %get-tuple-element.13.own_ref), custom_call_target="tpu_custom_call" | custom-call | tf_op jit(solution)/shard_map/pallas_call | solution.py:36
  (45 shorter events, 0.3 us)
Async XLA Ops:
  3.2 13.6 %copy-start.10 = (bf16[128,256]{1,0:T(8,128)(2,1)S(1)}, bf16[128,256]{1,0:T(8,128)(2,1)}, u32[]{:S(2)}) copy-start(bf16[128,256]{1,0:T(8,128)(2,1)} %param.15) | copy-start | bytes 196612
  3.2 13.6 %copy-start.11 = (bf16[128,256]{1,0:T(8,128)(2,1)S(1)}, bf16[128,256]{1,0:T(8,128)(2,1)}, u32[]{:S(2)}) copy-start(bf16[128,256]{1,0:T(8,128)(2,1)} %param.14) | copy-start | bytes 196612
  6.5 23.8 %all-to-all-start = ((bf16[16,8,1024]{2,1,0:T(8,128)(2,1)}), bf16[16,8,1024]{2,1,0:T(8,128)(2,1)S(1)}, u32[]{:S(2)}, u32[]{:S(2)}) async-start(bf16[16,8,1024]{2,1,0:T(8,128)(2,1)} %bitcast.36), calls=%async_computation | async-start | bytes 524288 | tf_op jit(solution)/shard_map/all_to_all | solution.py:28
  30.3 7.0 %copy-start.6 = (bf16[16,8,1024]{2,1,0:T(8,128)(2,1)}, bf16[16,8,1024]{2,1,0:T(8,128)(2,1)S(1)}, u32[]{:S(2)}) copy-start(bf16[16,8,1024]{2,1,0:T(8,128)(2,1)S(1)} %all-to-all-done.rows_ref) | copy-start | bytes 786436
  31.4 20.3 %all-to-all-start.1 = ((bf16[16,256,128]{2,1,0:T(8,128)(2,1)}), bf16[16,256,128]{2,1,0:T(8,128)(2,1)S(1)}, u32[]{:S(2)}, u32[]{:S(2)}) async-start(bf16[16,256,128]{2,1,0:T(8,128)(2,1)} %bitcast.9), calls=%async_computation.1 | async-start | bytes 2097152 | tf_op jit(solution)/shard_map/all_to_all | solution.py:28
  41.3 14.2 %copy-start.13 = (bf16[1,32,256]{2,1,0:T(8,128)(2,1)S(1)}, bf16[1,32,256]{2,1,0:T(8,128)(2,1)}, u32[]{:S(2)}) copy-start(bf16[1,32,256]{2,1,0:T(8,128)(2,1)} %param.17) | copy-start | bytes 49156
  41.3 14.2 %copy-start.14 = (bf16[1,32,256]{2,1,0:T(8,128)(2,1)S(1)}, bf16[1,32,256]{2,1,0:T(8,128)(2,1)}, u32[]{:S(2)}) copy-start(bf16[1,32,256]{2,1,0:T(8,128)(2,1)} %param.16) | copy-start | bytes 49156
  51.8 25.4 %copy-start.1 = (bf16[16,256,128]{2,1,0:T(8,128)(2,1)}, bf16[16,256,128]{2,1,0:T(8,128)(2,1)S(1)}, u32[]{:S(2)}) copy-start(bf16[16,256,128]{2,1,0:T(8,128)(2,1)S(1)} %all-to-all-done.1.kv_ref) | copy-start | bytes 3145732
  51.8 24.7 %all-to-all-start.2 = ((bf16[8,48,1024]{2,1,0:T(8,128)(2,1)}), bf16[8,48,1024]{2,1,0:T(8,128)(2,1)S(1)}, u32[]{:S(2)}, u32[]{:S(2)}) async-start(bf16[8,48,1024]{2,1,0:T(8,128)(2,1)} %shard_map.129), calls=%async_computation.2 | async-start | bytes 1572864 | tf_op jit(solution)/shard_map/all_to_all | solution.py:28
  55.5 43.1 %copy-start.8 = (bf16[32,512]{1,0:T(8,128)(2,1)}, bf16[32,512]{1,0:T(8,128)(2,1)S(1)}, u32[]{:S(2)}) copy-start(bf16[32,512]{1,0:T(8,128)(2,1)S(1)} %pad_maximum_fusion.1.own_ref) | copy-start | bytes 98308
  76.4 7.3 %copy-start.5 = (bf16[8,48,1024]{2,1,0:T(8,128)(2,1)}, bf16[8,48,1024]{2,1,0:T(8,128)(2,1)S(1)}, u32[]{:S(2)}) copy-start(bf16[8,48,1024]{2,1,0:T(8,128)(2,1)S(1)} %all-to-all-done.2.rows_ref) | copy-start | bytes 2359300
  77.2 21.4 %all-to-all-start.4 = ((bf16[8,32,512]{2,1,0:T(8,128)(2,1)}), bf16[8,32,512]{2,1,0:T(8,128)(2,1)S(1)}, u32[]{:S(2)}, u32[]{:S(2)}) async-start(bf16[8,32,512]{2,1,0:T(8,128)(2,1)} %broadcast_in_dim.173), calls=%async_computation.4 | async-start | bytes 524288 | tf_op jit(solution)/shard_map/all_to_all | solution.py:28
  98.6 21.1 %copy-start.7 = (bf16[8,32,512]{2,1,0:T(8,128)(2,1)}, bf16[8,32,512]{2,1,0:T(8,128)(2,1)S(1)}, u32[]{:S(2)}) copy-start(bf16[8,32,512]{2,1,0:T(8,128)(2,1)S(1)} %all-to-all-done.4.kv_ref) | copy-start | bytes 786436
  119.7 6.8 %copy-start.3 = (bf16[1,256,1792]{2,1,0:T(8,128)(2,1)S(1)}, bf16[1,256,1792]{2,1,0:T(8,128)(2,1)}, u32[]{:S(2)}) copy-start(bf16[1,256,1792]{2,1,0:T(8,128)(2,1)} %param.10) | copy-start | bytes 2752516
  119.7 34.8 %all-to-all-start.3 = ((bf16[128,8,512]{2,1,0:T(8,128)(2,1)}), bf16[128,8,512]{2,1,0:T(8,128)(2,1)S(1)}, u32[]{:S(2)}, u32[]{:S(2)}) async-start(bf16[128,8,512]{2,1,0:T(8,128)(2,1)} %get-tuple-element.12), calls=%async_computation.3 | async-start | bytes 2097152 | tf_op jit(solution)/shard_map/all_to_all | solution.py:28
  126.5 1.3 copy-start
  127.8 1.3 copy-start.12
  127.8 2.1 %copy-start.4 = (bf16[1,256,1792]{1,2,0:T(8,128)(2,1)S(1)}, bf16[1,256,1792]{1,2,0:T(8,128)(2,1)}, u32[]{:S(2)}) copy-start(bf16[1,256,1792]{1,2,0:T(8,128)(2,1)} %copy.37) | copy-start | bytes 2752516
  131.4 1.4 copy-start.9
  154.5 1.0 copy-start.2
